TPU v7x, 32 devices: a whole 2x2x4 slice. The times are simulated.
32 devices in a mesh: gz: 16 (over z, y, core), gy: 2 (over x).
Axes of the slice: x: 2, y: 2, z: 4, core: 2. Of those that a mesh axis runs over, the one named last changes fastest.
Arguments:
- fixed_image: float32 [160, 80, 320], P('gz', 'gy'), may hold values from -6 to 6
- moving_image: float32 [160, 80, 320], P('gz', 'gy'), may hold values from -6 to 6
- moving_grad: float32 [3, 160, 80, 320], P(None, 'gz', 'gy'), may hold values from -6 to 6
Outputs:
- control_grad: float32 [32, 3, 16, 64], P('gz', None, 'gy')
All inputs are finite; a program needn't handle non-finite values.
Results may differ from a plain program's by a relative error of at most 0.00016.
Values sent between devices are 32-bit elements; how exact they have to be, the bound alone decides.
A program may use at most 64 MiB of HBM per device.

v0:
```python
import functools

import jax
import jax.numpy as jnp
import numpy as np
from jax import lax
from jax.experimental import pallas as pl
from jax.experimental.pallas import tpu as pltpu
from jax.sharding import PartitionSpec as P

RADIUS = 4
SPACING = 5
EPS = 36.0
SIM_WEIGHT = 8.0
WINDOW = float((2 * RADIUS + 1) ** 3)
HALO = 2 * RADIUS
MESH = pl.DeviceIdType.MESH


def spline_weights(u):
    v = 1.0 - u
    return [
        v * v * v * (1.0 / 6.0),
        (3.0 * u * u * u - 6.0 * u * u + 4.0) * (1.0 / 6.0),
        (-3.0 * u * u * u + 3.0 * u * u + 3.0 * u + 1.0) * (1.0 / 6.0),
        u * u * u * (1.0 / 6.0),
    ]


def spline_matrix(voxels, points):
    position = np.arange(voxels)
    cell = position // SPACING
    u = (position - cell * SPACING) / SPACING
    weights = spline_weights(u)
    matrix = np.zeros((voxels, points))
    for k in range(4):
        np.add.at(matrix, (position, np.clip(cell - 1 + k, 0, points - 1)), weights[k])
    return matrix


def window_sum(v, axis, leading):
    n = v.shape[axis]

    def moved(a, s):
        return pltpu.roll(a, n - s if leading else s, axis)

    two = v + moved(v, 1)
    four = two + moved(two, 2)
    eight = four + moved(four, 4)
    return eight + moved(v, 8)


def split(v):
    hi = v.astype(jnp.bfloat16)
    return hi, (v - hi.astype(jnp.float32)).astype(jnp.bfloat16)


def dot(a, b):
    return jnp.dot(a, b, preferred_element_type=jnp.float32)


def kernel(
    gz_count, planes, height, width, points_y, points_x,
    fixed_ref, moving_ref, grad_ref, bx_hbm, by_hbm, band_hbm, out_ref,
    bx_ref, by_ref, band, raw, ext, grad, sums, boxes, coef, ksum, slope, acc, part, arrived,
    local_sem, z_send, z_recv, y_send, y_recv, p_send, p_recv,
):
    z, g = lax.axis_index("gz"), lax.axis_index("gy")
    other = 1 - g
    up, down = z < gz_count - 1, z > 0
    rows, lanes = slope.shape
    y0 = pl.multiple_of(g * HALO, 8)
    y_src = pl.multiple_of(jnp.where(g == 0, height - HALO, HALO), 8)
    y_dst = pl.multiple_of(jnp.where(g == 0, 0, height), 8)
    owned = planes // SPACING
    cols = owned + 3
    images = (fixed_ref, moving_ref)

    local = [pltpu.make_async_copy(images[i], raw.at[i], local_sem.at[i]) for i in range(2)]
    local.append(pltpu.make_async_copy(grad_ref, grad, local_sem.at[2]))
    tables = [
        pltpu.make_async_copy(band_hbm, band, local_sem.at[3]),
        pltpu.make_async_copy(bx_hbm, bx_ref, local_sem.at[4]),
        pltpu.make_async_copy(by_hbm.at[g], by_ref, local_sem.at[5]),
    ]

    for copy in (*local, *tables):
        copy.start()

    ext_planes, packed = ext.shape[0], ext.shape[2]
    ext[:, rows - 8 :, :] = jnp.zeros((ext_planes, 8, packed), jnp.float32)

    @pl.when(jnp.logical_not(down))
    def _():
        ext[0:HALO] = jnp.zeros((HALO, rows, packed), jnp.float32)

    @pl.when(jnp.logical_not(up))
    def _():
        ext[HALO + planes :] = jnp.zeros((HALO, rows, packed), jnp.float32)

    barrier = pltpu.get_barrier_semaphore()

    def greet(cond, dz, gy):
        @pl.when(cond)
        def _():
            pl.semaphore_signal(barrier, 1, device_id={"gz": z + dz, "gy": gy}, device_id_type=MESH)

    pl.semaphore_signal(barrier, 1, device_id={"gz": z, "gy": other}, device_id_type=MESH)
    for gy in (g, other):
        greet(up, 1, gy)
        greet(down, -1, gy)
    for i in range(2):
        local[i].wait()
    tail = width - 256

    @pl.loop(0, planes)
    def _(p):
        at = (HALO + p, pl.ds(y0, height))
        ext[(*at, slice(0, 256))] = raw[0, p, :, 0:256]
        ext[(*at, slice(256, 512))] = raw[1, p, :, 0:256]
        ext[(*at, slice(512, 640))] = jnp.concatenate(
            [raw[0, p, :, 256:width], raw[1, p, :, 256:width]], axis=1
        )

    pl.semaphore_wait(barrier, 1 + 2 * up.astype(jnp.int32) + 2 * down.astype(jnp.int32))

    def z_copy(d, s):
        src = HALO + planes - 1 - s if d == 0 else HALO + s
        dst = HALO - 1 - s if d == 0 else HALO + planes + s
        return pltpu.make_async_remote_copy(
            ext.at[src, pl.ds(y0, height)], ext.at[dst, pl.ds(y0, height)],
            z_send.at[d, s], z_recv.at[d, s],
            device_id={"gz": z + 1 if d == 0 else z - 1, "gy": g}, device_id_type=MESH,
        )

    def y_copy(at, d, s):
        return pltpu.make_async_remote_copy(
            ext.at[at, pl.ds(y_src, HALO)], ext.at[at, pl.ds(y_dst, HALO)],
            y_send.at[d, s], y_recv.at[d, s],
            device_id={"gz": z, "gy": other}, device_id_type=MESH,
        )

    y_own = y_copy(pl.ds(HALO, planes), 2, 0)

    def y_relay(d, s):
        return y_copy(HALO - 1 - s if d == 0 else HALO + planes + s, d, s)

    sends = (up, down)
    takes = (down, up)

    y_own.start()
    for s in range(HALO):
        for d in range(2):
            @pl.when(sends[d])
            def _():
                z_copy(d, s).start()
    y_own.wait_recv()
    tables[0].wait()

    def relay(s):
        for d in range(2):
            @pl.when(takes[d])
            def _():
                z_copy(d, s).wait_recv()
                y_relay(d, s).start()

    def ready(d, s):
        @pl.when(takes[d])
        def _():
            y_relay(d, s).wait_recv()

    in_tail = lax.broadcasted_iota(jnp.int32, (rows, 128), 1) < tail

    def plane(i, p):
        last = ext[p, :, 512:640]
        if i == 1:
            last = pltpu.roll(last, 128 - tail, 1)
        last = jnp.where(in_tail, last, 0.0)
        return jnp.concatenate([ext[p, :, 256 * i : 256 * (i + 1)], last], axis=1)

    def fields(p):
        f, m = plane(0, p), plane(1, p)
        return f, m, f * f, m * m, f * m

    row = lax.broadcasted_iota(jnp.int32, (rows, lanes), 0)
    lane = lax.broadcasted_iota(jnp.int32, (rows, lanes), 1)
    inside = (row >= RADIUS) & (row < rows - RADIUS) & (lane >= RADIUS) & (lane < width + RADIUS)

    def band_dots(v, at, mid, end):
        pieces = []
        for _ in range(3):
            piece = v.astype(jnp.bfloat16)
            v = v - piece.astype(jnp.float32)
            pieces.append(piece)
        left = sum(dot(p[:, 0:256], band[:, at:mid]) for p in pieces)
        right = sum(dot(p[:, 128:384], band[:, mid:end]) for p in pieces)
        return left, right

    def coefficients(way, k):
        left, right = band_dots(sums[way].reshape(5 * rows, lanes), 0, 256, 384)
        boxes[0 : 5 * rows, 0:256] = left
        boxes[0 : 5 * rows, 256:] = right
        sf, sm, sff, smm, sfm = (
            window_sum(boxes[i * rows : (i + 1) * rows], 0, False) for i in range(5)
        )
        cov = sfm - sf * sm * (1.0 / WINDOW)
        var_f = sff - sf * sf * (1.0 / WINDOW) + EPS
        var_m = smm - sm * sm * (1.0 / WINDOW) + EPS
        at = z * planes + k - RADIUS
        valid = (at >= 0) & (at < gz_count * planes)
        keep = jnp.where(valid, 1.0, 0.0)
        inv = 1.0 / (var_f * var_m)
        q = jnp.where(inside, cov * inv * keep, 0.0)
        h = q * cov * (var_f * inv)
        coef[0, k] = q
        coef[1, k] = h
        coef[2, k] = (q * sf - h * sm) * (1.0 / WINDOW)

    for i in range(5):
        sums[0, i] = jnp.zeros((rows, lanes), jnp.float32)

    @pl.loop(0, HALO + 1)
    def _(p):
        for i, v in enumerate(fields(HALO + p)):
            sums[0, i] += v

    sums[1] = sums[0]
    coefficients(0, HALO)

    def move(way, new, old, k):
        for i, (a, b) in enumerate(zip(fields(new), fields(old))):
            sums[way, i] += a - b
        coefficients(way, k)

    first = planes - 1 - HALO
    for j in range(first):
        move(0, 2 * HALO + 1 + j, HALO + j, HALO + 1 + j)

    acc[...] = jnp.zeros(acc.shape, jnp.float32)
    local[2].wait()

    def output(way, o, new, old):
        total = ksum[way] + coef[:, new] - coef[:, old]
        ksum[way] = total
        left, right = band_dots(total.reshape(3 * rows, lanes), 384, 512, 768)
        boxes[0 : 3 * rows, 0:128] = left
        boxes[0 : 3 * rows, 128:] = right
        boxed = [window_sum(boxes[i * rows : (i + 1) * rows], 0, True) for i in range(3)]
        slope[...] = (-2.0 * SIM_WEIGHT) * (
            plane(0, o + HALO) * boxed[0] - plane(1, o + HALO) * boxed[1] - boxed[2]
        )
        cell = lax.div(o, SPACING)
        weights = spline_weights((o - cell * SPACING).astype(jnp.float32) * (1.0 / SPACING))
        own = slope[pl.ds(y0, height), 0:width]
        for c in range(3):
            v = own * grad[c, o]
            for k in range(4):
                acc[c * cols + cell + k] += weights[k] * v

    meet = HALO - planes // 2
    relay(0)

    @pl.loop(0, HALO)
    def _(s):
        @pl.when(s < HALO - 1)
        def _():
            relay(s + 1)

        ready(0, s)
        move(1, HALO - 1 - s, 2 * HALO - s, HALO - 1 - s)
        ready(1, s)
        move(0, HALO + planes + s, planes - 1 + s, planes + s)

        @pl.when(s == meet)
        def _():
            for way, start in ((1, HALO - meet), (0, planes - HALO - 1 + meet)):
                ksum[way] = coef[:, start]

                @pl.loop(start + 1, start + HALO + 1)
                def _(k):
                    ksum[way] += coef[:, k]

        @pl.when(s >= meet)
        def _():
            low, high = HALO - 1 - s, planes - HALO + s
            output(1, low, low, low + HALO + 1)
            output(0, high, high + HALO, high - 1)

    tables[1].wait()
    tables[2].wait()
    for c in range(3):
        v = acc[c * cols : (c + 1) * cols].reshape(cols * height, width)
        hi, lo = split(v)
        along_x = dot(hi, bx_ref[0]) + dot(hi, bx_ref[1]) + dot(lo, bx_ref[0])
        hi, lo = split(along_x)
        by_hi, by_lo = by_ref[0], by_ref[1]
        along_y = dot(by_hi, hi) + dot(by_lo, hi) + dot(by_hi, lo)
        half = points_y // 2
        for j in range(cols):
            for h in range(2):
                at = j * points_y + h * half
                part[h, j, c] = along_y[at : at + half]

    @pl.when(jnp.logical_not(down))
    def _():
        part[:, 1] += part[:, 0]

    @pl.when(jnp.logical_not(up))
    def _():
        part[:, owned] += part[:, owned + 1] + part[:, owned + 2]

    def p_copy(slot, half, first_row, count, dz, gy):
        return pltpu.make_async_remote_copy(
            part.at[half, pl.ds(first_row, count)],
            arrived.at[slot, pl.ds(0, count)],
            p_send.at[slot], p_recv.at[slot],
            device_id={"gz": z + dz, "gy": gy}, device_id_type=MESH,
        )

    partner = p_copy(0, other, 1, owned, 0, other)
    ups = [p_copy(1, g, 1 + owned, 2, 1, g), p_copy(2, other, 1 + owned, 2, 1, other)]
    downs = [p_copy(3, g, 0, 1, -1, g), p_copy(4, other, 0, 1, -1, other)]

    @pl.when(up)
    def _():
        for copy in ups:
            copy.start()

    @pl.when(down)
    def _():
        for copy in downs:
            copy.start()

    partner.start()
    partner.wait_recv()
    out_ref[...] = part[g, 1 : 1 + owned] + arrived[0]

    @pl.when(down)
    def _():
        for copy in ups:
            copy.wait_recv()
        out_ref[0:2] += arrived[1, 0:2] + arrived[2, 0:2]

    @pl.when(up)
    def _():
        for copy in downs:
            copy.wait_recv()
        out_ref[owned - 1 : owned] += arrived[3, 0:1] + arrived[4, 0:1]

    partner.wait_send()
    y_own.wait_send()

    @pl.when(up)
    def _():
        for copy in ups:
            copy.wait_send()

    @pl.when(down)
    def _():
        for copy in downs:
            copy.wait_send()

    for d in range(2):
        @pl.when(sends[d])
        def _():
            for s in range(HALO):
                z_copy(d, s).wait_send()

        @pl.when(takes[d])
        def _():
            for s in range(HALO):
                y_relay(d, s).wait_send()


def hi_lo(matrix):
    hi = matrix.astype(jnp.bfloat16)
    lo = (matrix - hi.astype(np.float64)).astype(jnp.bfloat16)
    return np.stack([hi, lo])


def band_matrices():
    a, j = np.arange(256)[:, None], np.arange(384)[None, :]
    back = np.concatenate([(j - a)[:, :256], (j - a - 128)[:, 256:]], axis=1)
    ahead = np.concatenate([(a - j)[:, :128], (a + 128 - j)[:, 128:]], axis=1)
    shift = np.concatenate([back, ahead], axis=1)
    return ((shift >= 0) & (shift <= 2 * RADIUS)).astype(jnp.bfloat16)


def local(gz_count, gy_count, fixed_image, moving_image, moving_grad):
    planes, height, width = fixed_image.shape
    points_x, points_y = width // SPACING, gy_count * height // SPACING
    owned = planes // SPACING
    cols = owned + 3
    assert gy_count == 2 and planes >= HALO + 1 and owned >= 2 and height % 8 == 0
    bx = hi_lo(spline_matrix(width, points_x))
    by_all = spline_matrix(gy_count * height, points_y)
    by = np.stack(
        [hi_lo(np.kron(np.eye(cols), by_all[h * height : (h + 1) * height].T)) for h in range(2)]
    )
    rows = height + 2 * HALO
    lanes = (width + HALO + 127) // 128 * 128
    ext_planes = planes + 2 * HALO
    assert lanes == 384 and 256 < width <= 320 and planes % 2 == 0 and planes <= 2 * HALO
    band = band_matrices()
    f32 = jnp.float32
    body = functools.partial(kernel, gz_count, planes, height, width, points_y, points_x)
    vmem, hbm = (pl.BlockSpec(memory_space=m) for m in (pltpu.VMEM, pltpu.HBM))
    half = points_y // 2
    return pl.pallas_call(
        body,
        out_shape=jax.ShapeDtypeStruct((owned, 3, half, points_x), f32),
        in_specs=[hbm] * 6,
        out_specs=vmem,
        scratch_shapes=[
            pltpu.VMEM(bx.shape, jnp.bfloat16),
            pltpu.VMEM(by.shape[1:], jnp.bfloat16),
            pltpu.VMEM(band.shape, jnp.bfloat16),
            pltpu.VMEM((2, planes, height, width), f32),
            pltpu.VMEM((ext_planes, rows, 640), f32),
            pltpu.VMEM(moving_grad.shape, f32),
            pltpu.VMEM((2, 5, rows, lanes), f32),
            pltpu.VMEM((5 * rows, lanes), f32),
            pltpu.VMEM((3, planes + HALO, rows, lanes), f32),
            pltpu.VMEM((2, 3, rows, lanes), f32),
            pltpu.VMEM((rows, lanes), f32),
            pltpu.VMEM((3 * cols, height, width), f32),
            pltpu.VMEM((2, cols, 3, half, points_x), f32),
            pltpu.VMEM((5, owned, 3, half, points_x), f32),
            pltpu.SemaphoreType.DMA((6,)),
            pltpu.SemaphoreType.DMA((2, HALO)),
            pltpu.SemaphoreType.DMA((2, HALO)),
            pltpu.SemaphoreType.DMA((3, HALO)),
            pltpu.SemaphoreType.DMA((3, HALO)),
            pltpu.SemaphoreType.DMA((5,)),
            pltpu.SemaphoreType.DMA((5,)),
        ],
        compiler_params=pltpu.CompilerParams(
            collective_id=0, has_side_effects=True, vmem_limit_bytes=60 * 2**20
        ),
    )(fixed_image, moving_image, moving_grad, jnp.asarray(bx), jnp.asarray(by), jnp.asarray(band))


def solution(mesh):
    in_specs = (P("gz", "gy", None), P("gz", "gy", None), P(None, "gz", "gy", None))
    out_specs = P("gz", None, "gy", None)
    body = functools.partial(local, mesh.shape["gz"], mesh.shape["gy"])
    return jax.shard_map(body, mesh=mesh, in_specs=in_specs, out_specs=out_specs, check_vma=False)
```

profile of v0, /device:TPU:1, one launch (start us, length us, event | category | flops | bytes accessed | tf_op | source)
XLA Modules:
  0.0 42.0 jit_solution(12723513856492633157)
XLA Ops:
  0.0 40.6 %shard_map.64 = f32[2,3,8,64]{3,2,1,0:T(8,128)} custom-call(f32[10,40,320]{2,1,0:T(8,128)} %fixed_ref.1, f32[10,40,320]{2,1,0:T(8,128)} %moving_ref.1, f32[3,10,40,320]{3,2,1,0:T(8,128)} %grad_ref.1, bf16[2,320,64]{2,1,0:T(8,128)(2,1)} %constant.6.clone.bx_hbm, bf16[2,2,80,200]{3,2,1,0:T(8,128)(2,1)} %constant.7.clone.by_hbm, ...), custom_call_target="tpu_custom_call" | custom-call | tf_op jit(solution)/shard_map/pallas_call | solution.py:409
  40.6 1.3 %copy.8 = f32[2,3,8,64]{3,2,1,0:T(8,128)} copy(f32[2,3,8,64]{3,2,1,0:T(8,128)} %shard_map.64) | data formatting | bytes 24576
where the time goes:
time: 42.1 us; the launch traced here: 42 us
  Pallas kernels  40.6 us (96%)
  local copies, waits for them, and re-layouts  1.35 us (3%)
    pallas_call x1, Pallas kernels, local(): pl.pallas_call(body, out_shape=jax.ShapeDtypeStruct((owned, 3, half, poin...  40.6 us
    unnamed x1, local copies, waits for them, and re-layouts  1.35 us

commit v1 on v0

--- a/solution.py
+++ b/solution.py
@@ -62,19 +62,32 @@
 def kernel(
     gz_count, planes, height, width, points_y, points_x,
     fixed_ref, moving_ref, grad_ref, bx_hbm, by_hbm, band_hbm, out_ref,
-    bx_ref, by_ref, band, raw, ext, grad, sums, boxes, coef, ksum, slope, acc, part, arrived,
-    local_sem, z_send, z_recv, y_send, y_recv, p_send, p_recv,
+    bx_ref, by_ref, band, raw, ext, grad, sums, boxes, coef, ksum, full, slope, lent, owed, acc,
+    part, arrived,
+    local_sem, z_send, z_recv, y_send, y_recv, s_send, s_recv, p_send, p_recv,
 ):
     z, g = lax.axis_index("gz"), lax.axis_index("gy")
     other = 1 - g
     up, down = z < gz_count - 1, z > 0
-    rows, lanes = slope.shape
+    rows, lanes = full.shape
     y0 = pl.multiple_of(g * HALO, 8)
     y_src = pl.multiple_of(jnp.where(g == 0, height - HALO, HALO), 8)
     y_dst = pl.multiple_of(jnp.where(g == 0, 0, height), 8)
     owned = planes // SPACING
     cols = owned + 3
     images = (fixed_ref, moving_ref)
+
+    near = 1 - lax.rem(z, 2)
+    far = 1 - near
+
+    def has(d):
+        return d * (gz_count - 1 - z) + (1 - d) * z > 0
+
+    def edge(d, s):
+        return d * (planes - 1 - s) + (1 - d) * s
+
+    def beyond(d, s):
+        return d * (RADIUS + planes + s) + (1 - d) * (RADIUS - 1 - s)
 
     local = [pltpu.make_async_copy(images[i], raw.at[i], local_sem.at[i]) for i in range(2)]
     local.append(pltpu.make_async_copy(grad_ref, grad, local_sem.at[2]))
@@ -87,17 +100,6 @@
     for copy in (*local, *tables):
         copy.start()
 
-    ext_planes, packed = ext.shape[0], ext.shape[2]
-    ext[:, rows - 8 :, :] = jnp.zeros((ext_planes, 8, packed), jnp.float32)
-
-    @pl.when(jnp.logical_not(down))
-    def _():
-        ext[0:HALO] = jnp.zeros((HALO, rows, packed), jnp.float32)
-
-    @pl.when(jnp.logical_not(up))
-    def _():
-        ext[HALO + planes :] = jnp.zeros((HALO, rows, packed), jnp.float32)
-
     barrier = pltpu.get_barrier_semaphore()
 
     def greet(cond, dz, gy):
@@ -109,13 +111,26 @@
     for gy in (g, other):
         greet(up, 1, gy)
         greet(down, -1, gy)
+
+    ext_planes, packed = ext.shape[0], ext.shape[2]
+    ext[:, rows - 8 :, :] = jnp.zeros((ext_planes, 8, packed), jnp.float32)
+
+    @pl.when(jnp.logical_not(down))
+    def _():
+        ext[0:RADIUS] = jnp.zeros((RADIUS, rows, packed), jnp.float32)
+
+    @pl.when(jnp.logical_not(up))
+    def _():
+        ext[RADIUS + planes :] = jnp.zeros((RADIUS, rows, packed), jnp.float32)
+
+    acc[...] = jnp.zeros(acc.shape, jnp.float32)
     for i in range(2):
         local[i].wait()
     tail = width - 256
 
     @pl.loop(0, planes)
     def _(p):
-        at = (HALO + p, pl.ds(y0, height))
+        at = (RADIUS + p, pl.ds(y0, height))
         ext[(*at, slice(0, 256))] = raw[0, p, :, 0:256]
         ext[(*at, slice(256, 512))] = raw[1, p, :, 0:256]
         ext[(*at, slice(512, 640))] = jnp.concatenate(
@@ -125,12 +140,11 @@
     pl.semaphore_wait(barrier, 1 + 2 * up.astype(jnp.int32) + 2 * down.astype(jnp.int32))
 
     def z_copy(d, s):
-        src = HALO + planes - 1 - s if d == 0 else HALO + s
-        dst = HALO - 1 - s if d == 0 else HALO + planes + s
         return pltpu.make_async_remote_copy(
-            ext.at[src, pl.ds(y0, height)], ext.at[dst, pl.ds(y0, height)],
+            ext.at[RADIUS + edge(1 - d, s), pl.ds(y0, height)],
+            ext.at[beyond(d, s), pl.ds(y0, height)],
             z_send.at[d, s], z_recv.at[d, s],
-            device_id={"gz": z + 1 if d == 0 else z - 1, "gy": g}, device_id_type=MESH,
+            device_id={"gz": z + 1 - 2 * d, "gy": g}, device_id_type=MESH,
         )
 
     def y_copy(at, d, s):
@@ -140,32 +154,36 @@
             device_id={"gz": z, "gy": other}, device_id_type=MESH,
         )
 
-    y_own = y_copy(pl.ds(HALO, planes), 2, 0)
+    y_own = y_copy(pl.ds(RADIUS, planes), 2, 0)
 
     def y_relay(d, s):
-        return y_copy(HALO - 1 - s if d == 0 else HALO + planes + s, d, s)
-
-    sends = (up, down)
-    takes = (down, up)
+        return y_copy(beyond(d, s), d, s)
+
+    def s_copy(d, s):
+        lane = slice(0, 256) if s % 2 else slice(256, packed)
+        at = (1 - s // 2, slice(None), lane)
+        return pltpu.make_async_remote_copy(
+            lent.at[(1 - d, *at)], owed.at[(d, *at)],
+            s_send.at[d, s], s_recv.at[d, s],
+            device_id={"gz": z + 1 - 2 * d, "gy": g}, device_id_type=MESH,
+        )
+
+    for d in (far, near):
+        @pl.when(has(d))
+        def _():
+            for s in range(RADIUS):
+                z_copy(1 - d, s).start()
 
     y_own.start()
-    for s in range(HALO):
-        for d in range(2):
-            @pl.when(sends[d])
-            def _():
-                z_copy(d, s).start()
-    y_own.wait_recv()
-    tables[0].wait()
-
-    def relay(s):
-        for d in range(2):
-            @pl.when(takes[d])
-            def _():
-                z_copy(d, s).wait_recv()
-                y_relay(d, s).start()
+
+    def relay(d, s):
+        @pl.when(has(d))
+        def _():
+            z_copy(d, s).wait_recv()
+            y_relay(d, s).start()
 
     def ready(d, s):
-        @pl.when(takes[d])
+        @pl.when(has(d))
         def _():
             y_relay(d, s).wait_recv()
 
@@ -206,96 +224,151 @@
         cov = sfm - sf * sm * (1.0 / WINDOW)
         var_f = sff - sf * sf * (1.0 / WINDOW) + EPS
         var_m = smm - sm * sm * (1.0 / WINDOW) + EPS
-        at = z * planes + k - RADIUS
-        valid = (at >= 0) & (at < gz_count * planes)
-        keep = jnp.where(valid, 1.0, 0.0)
         inv = 1.0 / (var_f * var_m)
-        q = jnp.where(inside, cov * inv * keep, 0.0)
+        q = jnp.where(inside, cov * inv, 0.0)
         h = q * cov * (var_f * inv)
         coef[0, k] = q
         coef[1, k] = h
         coef[2, k] = (q * sf - h * sm) * (1.0 / WINDOW)
 
-    for i in range(5):
-        sums[0, i] = jnp.zeros((rows, lanes), jnp.float32)
-
-    @pl.loop(0, HALO + 1)
-    def _(p):
-        for i, v in enumerate(fields(HALO + p)):
-            sums[0, i] += v
-
-    sums[1] = sums[0]
-    coefficients(0, HALO)
-
     def move(way, new, old, k):
         for i, (a, b) in enumerate(zip(fields(new), fields(old))):
             sums[way, i] += a - b
         coefficients(way, k)
 
-    first = planes - 1 - HALO
-    for j in range(first):
-        move(0, 2 * HALO + 1 + j, HALO + j, HALO + 1 + j)
-
-    acc[...] = jnp.zeros(acc.shape, jnp.float32)
-    local[2].wait()
-
-    def output(way, o, new, old):
-        total = ksum[way] + coef[:, new] - coef[:, old]
-        ksum[way] = total
-        left, right = band_dots(total.reshape(3 * rows, lanes), 384, 512, 768)
+    def step(d, s):
+        k = d * (planes - RADIUS + s) + (1 - d) * (RADIUS - 1 - s)
+        drop = d * (planes - 1 + s - RADIUS) + (1 - d) * (RADIUS + HALO - s)
+        ready(d, s)
+        move(d, beyond(d, s), drop, k)
+
+    def gradient(d, p):
+        left, right = band_dots(ksum[d].reshape(3 * rows, lanes), 384, 512, 768)
         boxes[0 : 3 * rows, 0:128] = left
         boxes[0 : 3 * rows, 128:] = right
         boxed = [window_sum(boxes[i * rows : (i + 1) * rows], 0, True) for i in range(3)]
-        slope[...] = (-2.0 * SIM_WEIGHT) * (
-            plane(0, o + HALO) * boxed[0] - plane(1, o + HALO) * boxed[1] - boxed[2]
-        )
+        full[...] = (-2.0 * SIM_WEIGHT) * (
+            plane(0, p) * boxed[0] - plane(1, p) * boxed[1] - boxed[2]
+        )
+        return full[pl.ds(y0, height)]
+
+    in_low = lax.broadcasted_iota(jnp.int32, (height, 128), 1) < tail
+
+    def lend(d, s):
+        v = gradient(d, beyond(d, s))
+        at = 1 - s // 2
+        if s % 2:
+            lent[d, at, :, 0:256] = v[:, 0:256]
+            lent[d, at, :, 512:] = v[:, 256:]
+        else:
+            lent[d, at, :, 256:512] = v[:, 0:256]
+            lent[d, at, :, 512:] = jnp.where(
+                in_low, lent[d, at, :, 512:], pltpu.roll(v[:, 256:], tail, 1)
+            )
+        s_copy(1 - d, s).start()
+
+    def lend_all(d):
+        ksum[d] = coef[:, edge(d, 0)]
+        for s in range(RADIUS - 1, -1, -1):
+            @pl.when(has(d))
+            def _():
+                lend(d, s)
+            ksum[d] += coef[:, edge(d, RADIUS - s)]
+
+    def own(d, i):
+        slope[edge(d, i)] = gradient(d, RADIUS + edge(d, i))
+
+        @pl.when(i < RADIUS)
+        def _():
+            ksum[d] += coef[:, edge(d, RADIUS + 1 + i)]
+
+    def project(o):
+        v = jnp.concatenate([slope[o, :, 0:width] * grad[c, o] for c in range(3)], axis=0)
+        hi, lo = split(v)
+        along = dot(hi, bx_ref[0]) + dot(hi, bx_ref[1]) + dot(lo, bx_ref[0])
         cell = lax.div(o, SPACING)
         weights = spline_weights((o - cell * SPACING).astype(jnp.float32) * (1.0 / SPACING))
-        own = slope[pl.ds(y0, height), 0:width]
         for c in range(3):
-            v = own * grad[c, o]
             for k in range(4):
-                acc[c * cols + cell + k] += weights[k] * v
-
-    meet = HALO - planes // 2
-    relay(0)
-
-    @pl.loop(0, HALO)
+                acc[c * cols + cell + k] += weights[k] * along[c * height : (c + 1) * height]
+
+    def finish(d, s):
+        o = edge(d, s)
+
+        @pl.when(has(d))
+        def _():
+            s_copy(d, s).wait_recv()
+            at = 1 - s // 2
+            if s % 2:
+                slope[o, :, 0:256] += owed[d, at, :, 0:256]
+            else:
+                slope[o, :, 0:256] += owed[d, at, :, 256:512]
+                slope[o, :, 256:] += pltpu.roll(owed[d, at, :, 512:], 128 - tail, 1)
+                twin = edge(d, s + 1)
+                slope[twin, :, 256:] += owed[d, at, :, 512:]
+
+        if s % 2 == 0:
+            project(edge(d, s + 1))
+            project(o)
+
+    for s in range(RADIUS):
+        relay(near, s)
+    relay(far, 0)
+    y_own.wait_recv()
+    tables[0].wait()
+
+    for i in range(5):
+        sums[0, i] = jnp.zeros((rows, lanes), jnp.float32)
+
+    @pl.loop(0, HALO + 1)
+    def _(p):
+        for i, v in enumerate(fields(RADIUS + p)):
+            sums[0, i] += v
+
+    sums[1] = sums[0]
+    coefficients(0, RADIUS)
+    for j in range(planes - 1 - HALO):
+        move(1, RADIUS + HALO + 1 + j, RADIUS + j, RADIUS + 1 + j)
+
+    relay(far, 1)
+
+    @pl.loop(0, RADIUS)
     def _(s):
-        @pl.when(s < HALO - 1)
-        def _():
-            relay(s + 1)
-
-        ready(0, s)
-        move(1, HALO - 1 - s, 2 * HALO - s, HALO - 1 - s)
-        ready(1, s)
-        move(0, HALO + planes + s, planes - 1 + s, planes + s)
-
-        @pl.when(s == meet)
-        def _():
-            for way, start in ((1, HALO - meet), (0, planes - HALO - 1 + meet)):
-                ksum[way] = coef[:, start]
-
-                @pl.loop(start + 1, start + HALO + 1)
-                def _(k):
-                    ksum[way] += coef[:, k]
-
-        @pl.when(s >= meet)
-        def _():
-            low, high = HALO - 1 - s, planes - HALO + s
-            output(1, low, low, low + HALO + 1)
-            output(0, high, high + HALO, high - 1)
-
+        step(near, s)
+
+        @pl.when(s == 1)
+        def _():
+            relay(far, 2)
+
+    lend_all(near)
+    relay(far, 3)
+
+    @pl.loop(0, RADIUS)
+    def _(s):
+        step(far, s)
+
+    lend_all(far)
+    local[2].wait()
     tables[1].wait()
+    half_planes = planes // 2
+
+    @pl.loop(0, half_planes)
+    def _(i):
+        own(near, i)
+        own(far, i)
+
+    for d in (near, far):
+        project(edge(d, RADIUS))
+    for d in (near, far):
+        for s in range(RADIUS - 1, -1, -1):
+            finish(d, s)
+
     tables[2].wait()
+    half = points_y // 2
     for c in range(3):
-        v = acc[c * cols : (c + 1) * cols].reshape(cols * height, width)
-        hi, lo = split(v)
-        along_x = dot(hi, bx_ref[0]) + dot(hi, bx_ref[1]) + dot(lo, bx_ref[0])
-        hi, lo = split(along_x)
+        hi, lo = split(acc[c * cols : (c + 1) * cols].reshape(cols * height, points_x))
         by_hi, by_lo = by_ref[0], by_ref[1]
         along_y = dot(by_hi, hi) + dot(by_lo, hi) + dot(by_hi, lo)
-        half = points_y // 2
         for j in range(cols):
             for h in range(2):
                 at = j * points_y + h * half
@@ -361,15 +434,12 @@
             copy.wait_send()
 
     for d in range(2):
-        @pl.when(sends[d])
-        def _():
-            for s in range(HALO):
-                z_copy(d, s).wait_send()
-
-        @pl.when(takes[d])
-        def _():
-            for s in range(HALO):
+        @pl.when(has(d))
+        def _():
+            for s in range(RADIUS):
+                z_copy(1 - d, s).wait_send()
                 y_relay(d, s).wait_send()
+                s_copy(1 - d, s).wait_send()
 
 
 def hi_lo(matrix):
@@ -399,8 +469,8 @@
     )
     rows = height + 2 * HALO
     lanes = (width + HALO + 127) // 128 * 128
-    ext_planes = planes + 2 * HALO
-    assert lanes == 384 and 256 < width <= 320 and planes % 2 == 0 and planes <= 2 * HALO
+    ext_planes = planes + 2 * RADIUS
+    assert lanes == 384 and width == 320 and planes == HALO + 2
     band = band_matrices()
     f32 = jnp.float32
     body = functools.partial(kernel, gz_count, planes, height, width, points_y, points_x)
@@ -420,17 +490,22 @@
             pltpu.VMEM(moving_grad.shape, f32),
             pltpu.VMEM((2, 5, rows, lanes), f32),
             pltpu.VMEM((5 * rows, lanes), f32),
-            pltpu.VMEM((3, planes + HALO, rows, lanes), f32),
+            pltpu.VMEM((3, planes, rows, lanes), f32),
             pltpu.VMEM((2, 3, rows, lanes), f32),
             pltpu.VMEM((rows, lanes), f32),
-            pltpu.VMEM((3 * cols, height, width), f32),
+            pltpu.VMEM((planes, height, lanes), f32),
+            pltpu.VMEM((2, 2, height, 640), f32),
+            pltpu.VMEM((2, 2, height, 640), f32),
+            pltpu.VMEM((3 * cols, height, points_x), f32),
             pltpu.VMEM((2, cols, 3, half, points_x), f32),
             pltpu.VMEM((5, owned, 3, half, points_x), f32),
             pltpu.SemaphoreType.DMA((6,)),
-            pltpu.SemaphoreType.DMA((2, HALO)),
-            pltpu.SemaphoreType.DMA((2, HALO)),
-            pltpu.SemaphoreType.DMA((3, HALO)),
-            pltpu.SemaphoreType.DMA((3, HALO)),
+            pltpu.SemaphoreType.DMA((2, RADIUS)),
+            pltpu.SemaphoreType.DMA((2, RADIUS)),
+            pltpu.SemaphoreType.DMA((3, RADIUS)),
+            pltpu.SemaphoreType.DMA((3, RADIUS)),
+            pltpu.SemaphoreType.DMA((2, RADIUS)),
+            pltpu.SemaphoreType.DMA((2, RADIUS)),
             pltpu.SemaphoreType.DMA((5,)),
             pltpu.SemaphoreType.DMA((5,)),
         ],

time: 42.1 us -> 34 us (0.81)
  Pallas kernels: 40.6 us -> 32.5 us
    pallas_call x1, Pallas kernels: 40.6 us -> 32.5 us  [local(): pl.pallas_call(body, out_shape=jax.ShapeDtypeStruct((owned, 3, half, poin...]
where the time goes in v1:
time: 34 us; the launch traced here: 33.9 us
  Pallas kernels  32.5 us (96%)
  local copies, waits for them, and re-layouts  1.35 us (4%)
    pallas_call x1, Pallas kernels, local(): pl.pallas_call(body, out_shape=jax.ShapeDtypeStruct((owned, 3, half, poin...  32.5 us
    unnamed x1, local copies, waits for them, and re-layouts  1.35 us

profile of v1, /device:TPU:1, one launch (start us, length us, event | category | flops | bytes accessed | tf_op | source)
XLA Modules:
  0.0 33.9 jit_solution(9992830126919822805)
XLA Ops:
  0.0 32.5 %shard_map.64 = f32[2,3,8,64]{3,2,1,0:T(8,128)} custom-call(f32[10,40,320]{2,1,0:T(8,128)} %fixed_ref.1, f32[10,40,320]{2,1,0:T(8,128)} %moving_ref.1, f32[3,10,40,320]{3,2,1,0:T(8,128)} %grad_ref.1, bf16[2,320,64]{2,1,0:T(8,128)(2,1)} %constant.6.clone.bx_hbm, bf16[2,2,80,200]{3,2,1,0:T(8,128)(2,1)} %constant.7.clone.by_hbm, ...), custom_call_target="tpu_custom_call" | custom-call | tf_op jit(solution)/shard_map/pallas_call | solution.py:479
  32.5 1.3 %copy.8 = f32[2,3,8,64]{3,2,1,0:T(8,128)} copy(f32[2,3,8,64]{3,2,1,0:T(8,128)} %shard_map.64) | data formatting | bytes 24576

commit v2 on v1

v2 whole, which is shorter than its diff:
```python
import functools

import jax
import jax.numpy as jnp
import numpy as np
from jax import lax
from jax.experimental import pallas as pl
from jax.experimental.pallas import tpu as pltpu
from jax.sharding import PartitionSpec as P

RADIUS = 4
SPACING = 5
EPS = 36.0
SIM_WEIGHT = 8.0
WINDOW = float((2 * RADIUS + 1) ** 3)
HALO = 2 * RADIUS
LANES = 128
TILES = 3
MESH = pl.DeviceIdType.MESH


def spline_weights(u):
    v = 1.0 - u
    return [
        v * v * v * (1.0 / 6.0),
        (3.0 * u * u * u - 6.0 * u * u + 4.0) * (1.0 / 6.0),
        (-3.0 * u * u * u + 3.0 * u * u + 3.0 * u + 1.0) * (1.0 / 6.0),
        u * u * u * (1.0 / 6.0),
    ]


def spline_matrix(voxels, points):
    position = np.arange(voxels)
    cell = position // SPACING
    u = (position - cell * SPACING) / SPACING
    weights = spline_weights(u)
    matrix = np.zeros((voxels, points))
    for k in range(4):
        np.add.at(matrix, (position, np.clip(cell - 1 + k, 0, points - 1)), weights[k])
    return matrix


def split(v):
    hi = v.astype(jnp.bfloat16)
    return hi, (v - hi.astype(jnp.float32)).astype(jnp.bfloat16)


def turn(v, n):
    return pltpu.roll(v, n % LANES, 1)


def dot(a, b):
    return jnp.dot(a, b, preferred_element_type=jnp.float32)


def kernel(
    gz_count, planes, height, width, points_y, points_x,
    fixed_ref, moving_ref, grad_ref, bx_hbm, by_hbm, band_hbm, out_ref,
    bx_ref, by_ref, band, raw, ext, ends, flank, flank_ends, grad, sums, flank_sums, boxes, threes,
    coef, ksum, gboxes, gthrees, slope, lent, owed, acc, part, arrived,
    local_sem, z_send, z_recv, y_send, y_recv, s_send, s_recv, p_send, p_recv,
):
    z, g = lax.axis_index("gz"), lax.axis_index("gy")
    other = 1 - g
    up, down = z < gz_count - 1, z > 0
    rows = height + HALO
    y_src = pl.multiple_of(other * (height - HALO), 8)
    owned = planes // SPACING
    cols = owned + 3
    images = (fixed_ref, moving_ref)

    near = 1 - lax.rem(z, 2)
    far = 1 - near

    def has(d):
        return d * (gz_count - 1 - z) + (1 - d) * z > 0

    def edge(d, s):
        return d * (planes - 1 - s) + (1 - d) * s

    def beyond(d, s):
        return d * (RADIUS + planes + s) + (1 - d) * (RADIUS - 1 - s)

    local = [pltpu.make_async_copy(images[i], raw.at[i], local_sem.at[i]) for i in range(2)]
    local.append(pltpu.make_async_copy(grad_ref, grad, local_sem.at[2]))
    tables = [
        pltpu.make_async_copy(bx_hbm, bx_ref, local_sem.at[3]),
        pltpu.make_async_copy(by_hbm.at[g], by_ref, local_sem.at[4]),
        pltpu.make_async_copy(band_hbm, band, local_sem.at[5]),
    ]

    for copy in (*local, *tables):
        copy.start()

    barrier = pltpu.get_barrier_semaphore()

    def greet(cond, dz, gy):
        @pl.when(cond)
        def _():
            pl.semaphore_signal(barrier, 1, device_id={"gz": z + dz, "gy": gy}, device_id_type=MESH)

    pl.semaphore_signal(barrier, 1, device_id={"gz": z, "gy": other}, device_id_type=MESH)
    for gy in (g, other):
        greet(up, 1, gy)
        greet(down, -1, gy)

    packed = ext.shape[2]
    acc[...] = jnp.zeros(acc.shape, jnp.float32)
    extended = (ext, ends, flank, flank_ends)

    @pl.when(jnp.logical_not(down))
    def _():
        for ref in extended:
            ref[0:RADIUS] = jnp.zeros((RADIUS, *ref.shape[1:]), jnp.float32)

    @pl.when(jnp.logical_not(up))
    def _():
        for ref in extended:
            ref[RADIUS + planes :] = jnp.zeros((RADIUS, *ref.shape[1:]), jnp.float32)

    for i in range(2):
        local[i].wait()
    tail = width - 256

    def spread(images, last, p):
        last[p] = turn(images[p, :, 512:640], -tail)

    @pl.loop(0, planes)
    def _(p):
        at = RADIUS + p
        ext[at, :, 0:256] = raw[0, p, :, 0:256]
        ext[at, :, 256:512] = raw[1, p, :, 0:256]
        ext[at, :, 512:640] = jnp.concatenate(
            [raw[0, p, :, 256:width], raw[1, p, :, 256:width]], axis=1
        )
        spread(ext, ends, at)

    pl.semaphore_wait(barrier, 1 + 2 * up.astype(jnp.int32) + 2 * down.astype(jnp.int32))

    def z_copy(d, s):
        return pltpu.make_async_remote_copy(
            ext.at[RADIUS + edge(1 - d, s)], ext.at[beyond(d, s)],
            z_send.at[d, s], z_recv.at[d, s],
            device_id={"gz": z + 1 - 2 * d, "gy": g}, device_id_type=MESH,
        )

    def y_copy(at, d, s):
        return pltpu.make_async_remote_copy(
            ext.at[at, pl.ds(y_src, HALO)], flank.at[at],
            y_send.at[d, s], y_recv.at[d, s],
            device_id={"gz": z, "gy": other}, device_id_type=MESH,
        )

    y_own = y_copy(pl.ds(RADIUS, planes), 2, 0)

    def y_relay(d, s):
        return y_copy(beyond(d, s), d, s)

    def s_copy(d, s):
        lane = slice(0, 256) if s % 2 else slice(256, packed)
        at = (1 - s // 2, slice(None), lane)
        return pltpu.make_async_remote_copy(
            lent.at[(1 - d, *at)], owed.at[(d, *at)],
            s_send.at[d, s], s_recv.at[d, s],
            device_id={"gz": z + 1 - 2 * d, "gy": g}, device_id_type=MESH,
        )

    for d in (far, near):
        @pl.when(has(d))
        def _():
            for s in range(RADIUS):
                z_copy(1 - d, s).start()

    y_own.start()

    def relay(d, s):
        @pl.when(has(d))
        def _():
            z_copy(d, s).wait_recv()
            y_relay(d, s).start()
            spread(ext, ends, beyond(d, s))

    def relayed(d, s):
        @pl.when(has(d))
        def _():
            y_relay(d, s).wait_recv()
            spread(flank, flank_ends, beyond(d, s))

    main = (ext, ends, sums)
    side = (flank, flank_ends, flank_sums)

    def tile(region, i, p, j):
        images, last, _ = region
        if j < 2:
            return images[p, :, 256 * i + LANES * j : 256 * i + LANES * (j + 1)]
        return last[p] if i else images[p, :, 512:640]

    def fields(region, p, j):
        f, m = (tile(region, i, p, j) for i in range(2))
        return f, m, f * f, m * m, f * m

    def lane_windows(tiles, count, leading):
        pieces = []
        for j in range(TILES):
            v, parts = tiles[j], []
            for _ in range(count):
                piece = v.astype(jnp.bfloat16)
                v = v - piece.astype(jnp.float32)
                parts.append(piece)
            pieces.append(parts)

        def product(j, at, lanes):
            weights = band[:, at : at + lanes]
            return sum(
                dot(jnp.concatenate([a, b], axis=1), weights)
                for a, b in zip(pieces[j], pieces[j + 1])
            )

        if leading:
            low, high = product(0, 384, 128), product(1, 512, 256)
            return low, high[:, 0:128], high[:, 128:]
        low, high = product(0, 0, 256), product(1, 256, 128)
        return low[:, 0:128], low[:, 128:], high

    row = lax.broadcasted_iota(jnp.int32, (rows, LANES), 0) + (g * height - RADIUS)
    lane = lax.broadcasted_iota(jnp.int32, (rows, LANES), 1) - RADIUS
    in_rows = (row >= 0) & (row < 2 * height)

    def first_sums(region):
        total = region[2]
        for j in range(TILES):
            def add(p, totals):
                return tuple(a + b for a, b in zip(totals, fields(region, RADIUS + p, j)))

            totals = lax.fori_loop(1, HALO + 1, add, fields(region, RADIUS, j))
            for i in range(5):
                total[0, i, j] = totals[i]
                total[1, i, j] = totals[i]

    def shift(region, way, new, old):
        total = region[2]
        for j in range(TILES):
            for i, (a, b) in enumerate(zip(fields(region, new, j), fields(region, old, j))):
                total[way, i, j] += a - b

    def middle(region):
        for j in range(planes - 1 - HALO):
            shift(region, 1, RADIUS + HALO + 1 + j, RADIUS + j)

    def centre(d, s):
        return d * (planes - RADIUS + s) + (1 - d) * (RADIUS - 1 - s)

    def advance(region, d, s):
        drop = d * (planes - 1 + s - RADIUS) + (1 - d) * (RADIUS + HALO - s)
        shift(region, d, beyond(d, s), drop)

    def totals_of(region, way):
        return [region[2][way, :, j].reshape(-1, LANES) for j in range(TILES)]

    def widen(k, way):
        wide = lane_windows(totals_of(main, way), 3, False)
        for j in range(TILES):
            for i in range(5):
                boxes[k, i, j, HALO : HALO + height] = wide[j][i * height : (i + 1) * height]

    def widen_flanks(centres, totals):
        n = 5 * HALO
        stacked = [jnp.concatenate([t[j] for t in totals], axis=0) for j in range(TILES)]
        wide = lane_windows(stacked, 3, False)
        for at, k in enumerate(centres):
            for j in range(TILES):
                for i in range(5):
                    v = wide[j][at * n + i * HALO : at * n + (i + 1) * HALO]
                    boxes[k, i, j, 0:HALO] = jnp.where(g == 0, 0.0, v)
                    boxes[k, i, j, HALO + height : rows + HALO] = jnp.where(g == 0, v, 0.0)

    def coefficients(k):
        for j in range(TILES):
            boxed = []
            for i in range(5):
                count = rows + 8
                v = boxes.at[k, i, j]
                threes[i, j] = v[0:count] + v[1 : count + 1] + v[2 : count + 2]
                v = threes.at[i, j]
                boxed.append(v[0:rows] + v[3 : rows + 3] + v[6 : rows + 6])
            sf, sm, sff, smm, sfm = boxed
            cov = sfm - sf * sm * (1.0 / WINDOW)
            var_f = sff - sf * sf * (1.0 / WINDOW) + EPS
            var_m = smm - sm * sm * (1.0 / WINDOW) + EPS
            x = lane + LANES * j
            inside = in_rows & (x >= 0) & (x < width)
            inv = 1.0 / (var_f * var_m)
            q = jnp.where(inside, cov * inv, 0.0)
            h = q * cov * (var_f * inv)
            coef[0, k, j] = q
            coef[1, k, j] = h
            coef[2, k, j] = (q * sf - h * sm) * (1.0 / WINDOW)

    spot = lax.broadcasted_iota(jnp.int32, (height, LANES), 1)

    def gradient(slot, p):
        wide = lane_windows([ksum[slot, :, j].reshape(3 * rows, LANES) for j in range(TILES)], 2, True)
        tiles = []
        for j in range(TILES):
            boxed = []
            for i in range(3):
                gboxes[slot, i, j, 0:rows] = wide[j][i * rows : (i + 1) * rows]
                v = gboxes.at[slot, i, j]
                gthrees[slot, i, j] = v[0:rows] + v[1 : rows + 1] + v[2 : rows + 2]
                v = gthrees.at[slot, i, j]
                boxed.append(v[0:height] + v[3 : height + 3] + v[6 : height + 6])
            f, m = (tile(main, i, p, j) for i in range(2))
            tiles.append((-2.0 * SIM_WEIGHT) * (f * boxed[0] - m * boxed[1] - boxed[2]))
        return tiles

    def gather(slot, d, s):
        for i in range(3):
            for j in range(TILES):
                ksum[slot, i, j] += coef[i, edge(d, s), j]

    def lend_all(slot, d):
        for i in range(3):
            ksum[slot, i] = coef[i, edge(d, 0)]

        @pl.when(has(d))
        def _():
            for s in range(RADIUS - 1, -1, -1):
                a, b, c = gradient(slot, beyond(d, s))
                at = 1 - s // 2
                if s % 2:
                    lent[d, at, :, 0:128] = a
                    lent[d, at, :, 128:256] = b
                    first = c
                else:
                    lent[d, at, :, 256:384] = a
                    lent[d, at, :, 384:512] = b
                    lent[d, at, :, 512:] = jnp.where(spot < tail, first, turn(c, tail))
                s_copy(1 - d, s).start()
                gather(slot, d, RADIUS - s)

        @pl.when(jnp.logical_not(has(d)))
        def _():
            for s in range(RADIUS):
                gather(slot, d, RADIUS - s)

    def own(slot, d, i):
        o = edge(d, i)
        for j, v in enumerate(gradient(slot, RADIUS + o)):
            slope[o, j] = v

    def project(o):
        v = jnp.concatenate(
            [
                jnp.concatenate(
                    [
                        slope[o, 0] * grad[c, o, :, 0:128],
                        slope[o, 1] * grad[c, o, :, 128:256],
                        slope[o, 2, :, 0:tail] * grad[c, o, :, 256:width],
                    ],
                    axis=1,
                )
                for c in range(3)
            ],
            axis=0,
        )
        hi = v.astype(jnp.bfloat16).astype(jnp.float32)
        v = jnp.concatenate([v, v - hi], axis=0).astype(jnp.bfloat16)
        both = dot(v, bx_ref[...])
        along = both[0 : 3 * height] + both[3 * height :]
        cell = lax.div(o, SPACING)
        weights = spline_weights((o - cell * SPACING).astype(jnp.float32) * (1.0 / SPACING))
        for c in range(3):
            for k in range(4):
                acc[c * cols + cell + k] += weights[k] * along[c * height : (c + 1) * height]

    def finish(d, s):
        o = edge(d, s)

        @pl.when(has(d))
        def _():
            s_copy(d, s).wait_recv()
            at = 1 - s // 2
            if s % 2:
                slope[o, 0] += owed[d, at, :, 0:128]
                slope[o, 1] += owed[d, at, :, 128:256]
            else:
                slope[o, 0] += owed[d, at, :, 256:384]
                slope[o, 1] += owed[d, at, :, 384:512]
                slope[o, 2] += turn(owed[d, at, :, 512:], -tail)
                slope[edge(d, s + 1), 2] += owed[d, at, :, 512:]

        if s % 2 == 0:
            project(edge(d, s + 1))
            project(o)

    tables[2].wait()
    first_sums(main)
    widen(RADIUS, 0)
    middle(main)
    widen(RADIUS + 1, 1)
    for s in range(RADIUS):
        relay(near, s)

    @pl.loop(0, RADIUS // 2)
    def _(i):
        for s in (2 * i, 2 * i + 1):
            advance(main, near, s)
            widen(centre(near, s), near)

    def far_own(s):
        relay(far, s)
        advance(main, far, s)
        widen(centre(far, s), far)

    far_own(0)
    y_own.wait_recv()

    @pl.loop(RADIUS, RADIUS + planes)
    def _(p):
        spread(flank, flank_ends, p)

    for s in range(RADIUS):
        relayed(near, s)
    first_sums(side)
    totals = [totals_of(side, 0)]
    middle(side)
    totals.append(totals_of(side, 1))
    for s in range(RADIUS):
        advance(side, near, s)
        totals.append(totals_of(side, near))
    widen_flanks(
        [RADIUS, RADIUS + 1, *(centre(near, s) for s in range(RADIUS))], totals
    )

    @pl.loop(0, RADIUS + 2)
    def _(i):
        coefficients(near * (RADIUS + i) + far * (RADIUS + 1 - i))

    far_own(1)
    lend_all(0, near)
    far_own(2)
    own(0, near, 0)
    gather(0, near, RADIUS + 1)
    own(0, near, 1)
    far_own(3)

    def far_flanks(steps):
        totals = []
        for s in steps:
            relayed(far, s)
            advance(side, far, s)
            totals.append(totals_of(side, far))
        widen_flanks([centre(far, s) for s in steps], totals)
        for s in steps:
            coefficients(centre(far, s))

    far_flanks([0, 1, 2])
    far_flanks([3])
    lend_all(1, far)
    local[2].wait()
    tables[0].wait()

    @pl.loop(2, planes // 2)
    def _(i):
        gather(0, near, RADIUS + i)
        own(0, near, i)
        own(1, far, i - 2)
        gather(1, far, RADIUS - 1 + i)

    own(1, far, planes // 2 - 2)
    gather(1, far, planes - 2)
    own(1, far, planes // 2 - 1)

    for d in (near, far):
        project(edge(d, RADIUS))
    for d in (near, far):
        for s in range(RADIUS - 2, -1, -2):
            finish(d, s + 1)
            finish(d, s)

    tables[1].wait()
    half = points_y // 2
    pieces = [split(acc[c * cols : (c + 1) * cols].reshape(cols * height, LANES)) for c in range(3)]
    along_y = sum(
        dot(by_ref[...], jnp.concatenate([piece[i] for piece in pieces], axis=1)) for i in range(2)
    )
    along_y = along_y[0 : cols * points_y] + along_y[cols * points_y :]
    for c in range(3):
        v = along_y[:, c * LANES : (c + 1) * LANES]
        v = (v + turn(v, LANES // 2))[:, 0:points_x]
        for j in range(cols):
            for h in range(2):
                at = j * points_y + h * half
                part[h, j, c] = v[at : at + half]

    @pl.when(jnp.logical_not(down))
    def _():
        part[:, 1] += part[:, 0]

    @pl.when(jnp.logical_not(up))
    def _():
        part[:, owned] += part[:, owned + 1] + part[:, owned + 2]

    def p_copy(slot, half, first_row, count, dz, gy):
        return pltpu.make_async_remote_copy(
            part.at[half, pl.ds(first_row, count)],
            arrived.at[slot, pl.ds(0, count)],
            p_send.at[slot], p_recv.at[slot],
            device_id={"gz": z + dz, "gy": gy}, device_id_type=MESH,
        )

    partner = p_copy(0, other, 1, owned, 0, other)
    ups = [p_copy(1, g, 1 + owned, 2, 1, g), p_copy(2, other, 1 + owned, 2, 1, other)]
    downs = [p_copy(3, g, 0, 1, -1, g), p_copy(4, other, 0, 1, -1, other)]

    @pl.when(up)
    def _():
        for copy in ups:
            copy.start()

    @pl.when(down)
    def _():
        for copy in downs:
            copy.start()

    partner.start()
    partner.wait_recv()
    out_ref[...] = part[g, 1 : 1 + owned] + arrived[0]

    @pl.when(down)
    def _():
        for copy in ups:
            copy.wait_recv()
        out_ref[0:2] += arrived[1, 0:2] + arrived[2, 0:2]

    @pl.when(up)
    def _():
        for copy in downs:
            copy.wait_recv()
        out_ref[owned - 1 : owned] += arrived[3, 0:1] + arrived[4, 0:1]

    partner.wait_send()
    y_own.wait_send()

    @pl.when(up)
    def _():
        for copy in ups:
            copy.wait_send()

    @pl.when(down)
    def _():
        for copy in downs:
            copy.wait_send()

    for d in range(2):
        @pl.when(has(d))
        def _():
            for s in range(RADIUS):
                z_copy(1 - d, s).wait_send()
                y_relay(d, s).wait_send()
                s_copy(1 - d, s).wait_send()


def hi_lo(matrix):
    hi = matrix.astype(jnp.bfloat16)
    lo = (matrix - hi.astype(np.float64)).astype(jnp.bfloat16)
    return np.stack([hi, lo])


def band_matrices(width):
    a, j = np.arange(256)[:, None], np.arange(384)[None, :]
    back = np.concatenate([(j - a)[:, :256], (j - a - 128)[:, 256:]], axis=1)
    ahead = np.concatenate([(a - j)[:, :128], (a + 128 - j)[:, 128:]], axis=1)
    shift = np.concatenate([back, ahead], axis=1)
    keep = (shift >= 0) & (shift <= 2 * RADIUS)
    keep[width - LANES :, 256:384] = False
    return keep.astype(jnp.bfloat16)


def local(gz_count, gy_count, fixed_image, moving_image, moving_grad):
    planes, height, width = fixed_image.shape
    points_x, points_y = width // SPACING, gy_count * height // SPACING
    owned = planes // SPACING
    cols = owned + 3
    assert gy_count == 2 and planes >= HALO + 1 and owned >= 2 and height % 8 == 0
    bx = np.concatenate(list(hi_lo(spline_matrix(width, points_x))), axis=1)
    by_all = spline_matrix(gy_count * height, points_y)
    by = np.stack(
        [
            np.concatenate(list(hi_lo(np.kron(np.eye(cols), by_all[h * height : (h + 1) * height].T))))
            for h in range(2)
        ]
    )
    rows = height + HALO
    ext_planes = planes + 2 * RADIUS
    band = band_matrices(width)
    assert width == 320 and points_x == 64 and planes == HALO + 2
    f32 = jnp.float32
    body = functools.partial(kernel, gz_count, planes, height, width, points_y, points_x)
    vmem, hbm = (pl.BlockSpec(memory_space=m) for m in (pltpu.VMEM, pltpu.HBM))
    half = points_y // 2
    return pl.pallas_call(
        body,
        out_shape=jax.ShapeDtypeStruct((owned, 3, half, points_x), f32),
        in_specs=[hbm] * 6,
        out_specs=vmem,
        scratch_shapes=[
            pltpu.VMEM(bx.shape, jnp.bfloat16),
            pltpu.VMEM(by.shape[1:], jnp.bfloat16),
            pltpu.VMEM(band.shape, jnp.bfloat16),
            pltpu.VMEM((2, planes, height, width), f32),
            pltpu.VMEM((ext_planes, height, 640), f32),
            pltpu.VMEM((ext_planes, height, LANES), f32),
            pltpu.VMEM((ext_planes, HALO, 640), f32),
            pltpu.VMEM((ext_planes, HALO, LANES), f32),
            pltpu.VMEM(moving_grad.shape, f32),
            pltpu.VMEM((2, 5, TILES, height, LANES), f32),
            pltpu.VMEM((2, 5, TILES, HALO, LANES), f32),
            pltpu.VMEM((planes, 5, TILES, rows + 2 * HALO, LANES), f32),
            pltpu.VMEM((5, TILES, rows + HALO, LANES), f32),
            pltpu.VMEM((3, planes, TILES, rows, LANES), f32),
            pltpu.VMEM((2, 3, TILES, rows, LANES), f32),
            pltpu.VMEM((2, 3, TILES, rows + HALO, LANES), f32),
            pltpu.VMEM((2, 3, TILES, rows, LANES), f32),
            pltpu.VMEM((planes, TILES, height, LANES), f32),
            pltpu.VMEM((2, 2, height, 640), f32),
            pltpu.VMEM((2, 2, height, 640), f32),
            pltpu.VMEM((3 * cols, height, LANES), f32),
            pltpu.VMEM((2, cols, 3, half, points_x), f32),
            pltpu.VMEM((5, owned, 3, half, points_x), f32),
            pltpu.SemaphoreType.DMA((6,)),
            pltpu.SemaphoreType.DMA((2, RADIUS)),
            pltpu.SemaphoreType.DMA((2, RADIUS)),
            pltpu.SemaphoreType.DMA((3, RADIUS)),
            pltpu.SemaphoreType.DMA((3, RADIUS)),
            pltpu.SemaphoreType.DMA((2, RADIUS)),
            pltpu.SemaphoreType.DMA((2, RADIUS)),
            pltpu.SemaphoreType.DMA((5,)),
            pltpu.SemaphoreType.DMA((5,)),
        ],
        compiler_params=pltpu.CompilerParams(
            collective_id=0, has_side_effects=True, vmem_limit_bytes=56450000
        ),
    )(fixed_image, moving_image, moving_grad, jnp.asarray(bx), jnp.asarray(by), jnp.asarray(band))


def solution(mesh):
    in_specs = (P("gz", "gy", None), P("gz", "gy", None), P(None, "gz", "gy", None))
    out_specs = P("gz", None, "gy", None)
    body = functools.partial(local, mesh.shape["gz"], mesh.shape["gy"])
    return jax.shard_map(body, mesh=mesh, in_specs=in_specs, out_specs=out_specs, check_vma=False)
```

time: 34 us -> 31.5 us (0.926); the launches traced: 33.9 us -> 30.9 us
  Pallas kernels: 32.5 us -> 29.4 us
    pallas_call x1, Pallas kernels: 32.5 us -> 29.4 us  [local(): pl.pallas_call(body, out_shape=jax.ShapeDtypeStruct((owned, 3, half, poin...]
    unnamed x1 -> x3, local copies, waits for them, and re-layouts: 1.35 us -> 1.5 us
where the time goes in v2:
time: 31.5 us; the launch traced here: 30.9 us
  Pallas kernels  29.4 us (93%)
  local copies, waits for them, and re-layouts  1.5 us (5%)
    pallas_call x1, Pallas kernels, local(): pl.pallas_call(body, out_shape=jax.ShapeDtypeStruct((owned, 3, half, poin...  29.4 us
    unnamed x3, local copies, waits for them, and re-layouts  1.5 us

profile of v2, /device:TPU:1, one launch (start us, length us, event | category | flops | bytes accessed | tf_op | source)
XLA Modules:
  0.0 30.9 jit_solution(17192626376978196035)
XLA Ops:
  0.0 0.0 copy-start
  0.0 0.9 %copy-done = bf16[320,128]{1,0:T(8,128)(2,1)S(1)} copy-done((bf16[320,128]{1,0:T(8,128)(2,1)S(1)}, bf16[320,128]{1,0:T(8,128)(2,1)}, u32[]{:S(2)}) %copy-start) | copy-done | bytes 81944
  0.9 29.4 %shard_map.64 = f32[2,3,8,64]{3,2,1,0:T(8,128)S(1)} custom-call(f32[10,40,320]{2,1,0:T(8,128)} %fixed_ref.1, f32[10,40,320]{2,1,0:T(8,128)} %moving_ref.1, f32[3,10,40,320]{3,2,1,0:T(8,128)} %grad_ref.1, bf16[320,128]{1,0:T(8,128)(2,1)S(1)} %copy-done, bf16[2,160,200]{2,1,0:T(8,128)(2,1)} %constant.7.clone.by_hbm, bf16[256,768]{1,0:T(8,128)(2,1)} %constant.8.clone.band_hbm), custom_call_target="tpu_custom_call" | custom-call | tf_op jit(solution)/shard_map/pallas_call | solution.py:602
  30.3 0.6 %copy.8 = f32[2,3,8,64]{3,2,1,0:T(8,128)} copy(f32[2,3,8,64]{3,2,1,0:T(8,128)S(1)} %shard_map.64) | data formatting | bytes 24576
Async XLA Ops:
  0.0 0.9 %copy-start = (bf16[320,128]{1,0:T(8,128)(2,1)S(1)}, bf16[320,128]{1,0:T(8,128)(2,1)}, u32[]{:S(2)}) copy-start(bf16[320,128]{1,0:T(8,128)(2,1)} %constant.6.clone.bx_hbm) | copy-start | bytes 245764

commit v3 on v2

--- a/solution.py
+++ b/solution.py
@@ -57,8 +57,8 @@
     gz_count, planes, height, width, points_y, points_x,
     fixed_ref, moving_ref, grad_ref, bx_hbm, by_hbm, band_hbm, out_ref,
     bx_ref, by_ref, band, raw, ext, ends, flank, flank_ends, grad, sums, flank_sums, boxes, threes,
-    coef, ksum, gboxes, gthrees, slope, lent, owed, acc, part, arrived,
-    local_sem, z_send, z_recv, y_send, y_recv, s_send, s_recv, p_send, p_recv,
+    coef, ksum, gboxes, gthrees, slope, lent, owed, projected, part, arrived,
+    local_sem, z_send, z_recv, y_send, y_recv, f_send, f_recv, s_send, s_recv, p_send, p_recv,
 ):
     z, g = lax.axis_index("gz"), lax.axis_index("gy")
     other = 1 - g
@@ -85,7 +85,7 @@
     local.append(pltpu.make_async_copy(grad_ref, grad, local_sem.at[2]))
     tables = [
         pltpu.make_async_copy(bx_hbm, bx_ref, local_sem.at[3]),
-        pltpu.make_async_copy(by_hbm.at[g], by_ref, local_sem.at[4]),
+        pltpu.make_async_copy(by_hbm.at[g, near], by_ref, local_sem.at[4]),
         pltpu.make_async_copy(band_hbm, band, local_sem.at[5]),
     ]
 
@@ -105,7 +105,6 @@
         greet(down, -1, gy)
 
     packed = ext.shape[2]
-    acc[...] = jnp.zeros(acc.shape, jnp.float32)
     extended = (ext, ends, flank, flank_ends)
 
     @pl.when(jnp.logical_not(down))
@@ -125,15 +124,13 @@
     def spread(images, last, p):
         last[p] = turn(images[p, :, 512:640], -tail)
 
-    @pl.loop(0, planes)
-    def _(p):
+    for p in range(planes):
         at = RADIUS + p
         ext[at, :, 0:256] = raw[0, p, :, 0:256]
         ext[at, :, 256:512] = raw[1, p, :, 0:256]
         ext[at, :, 512:640] = jnp.concatenate(
             [raw[0, p, :, 256:width], raw[1, p, :, 256:width]], axis=1
         )
-        spread(ext, ends, at)
 
     pl.semaphore_wait(barrier, 1 + 2 * up.astype(jnp.int32) + 2 * down.astype(jnp.int32))
 
@@ -151,10 +148,26 @@
             device_id={"gz": z, "gy": other}, device_id_type=MESH,
         )
 
-    y_own = y_copy(pl.ds(RADIUS, planes), 2, 0)
+    y_own = [
+        y_copy(pl.ds(RADIUS + near * (planes - RADIUS), RADIUS), 2, 0),
+        y_copy(pl.ds(RADIUS + far * RADIUS, planes - RADIUS), 2, 1),
+    ]
 
     def y_relay(d, s):
         return y_copy(beyond(d, s), d, s)
+
+    def forward(d, src, dst):
+        return pltpu.make_async_remote_copy(
+            flank.at[src], flank.at[dst], f_send.at[d], f_recv.at[d],
+            device_id={"gz": z + 1 - 2 * d, "gy": g}, device_id_type=MESH,
+        )
+
+    def forward_near(d):
+        src = RADIUS + (1 - d) * (planes - RADIUS)
+        return forward(d, pl.ds(src, RADIUS), pl.ds(d * (RADIUS + planes), RADIUS))
+
+    def forward_far(d):
+        return forward(d, RADIUS + edge(1 - d, RADIUS - 1), beyond(d, RADIUS - 1))
 
     def s_copy(d, s):
         lane = slice(0, 256) if s % 2 else slice(256, packed)
@@ -165,26 +178,24 @@
             device_id={"gz": z + 1 - 2 * d, "gy": g}, device_id_type=MESH,
         )
 
+    for copy in y_own:
+        copy.start()
     for d in (far, near):
         @pl.when(has(d))
         def _():
             for s in range(RADIUS):
                 z_copy(1 - d, s).start()
 
-    y_own.start()
+    for p in range(planes):
+        spread(ext, ends, RADIUS + p)
 
     def relay(d, s):
         @pl.when(has(d))
         def _():
             z_copy(d, s).wait_recv()
-            y_relay(d, s).start()
+            if s < RADIUS - 1:
+                y_relay(d, s).start()
             spread(ext, ends, beyond(d, s))
-
-    def relayed(d, s):
-        @pl.when(has(d))
-        def _():
-            y_relay(d, s).wait_recv()
-            spread(flank, flank_ends, beyond(d, s))
 
     main = (ext, ends, sums)
     side = (flank, flank_ends, flank_sums)
@@ -348,7 +359,7 @@
         for j, v in enumerate(gradient(slot, RADIUS + o)):
             slope[o, j] = v
 
-    def project(o):
+    def project(slots, planes_of):
         v = jnp.concatenate(
             [
                 jnp.concatenate(
@@ -359,19 +370,22 @@
                     ],
                     axis=1,
                 )
+                for o in planes_of
                 for c in range(3)
             ],
             axis=0,
         )
         hi = v.astype(jnp.bfloat16).astype(jnp.float32)
+        n = v.shape[0]
         v = jnp.concatenate([v, v - hi], axis=0).astype(jnp.bfloat16)
         both = dot(v, bx_ref[...])
-        along = both[0 : 3 * height] + both[3 * height :]
-        cell = lax.div(o, SPACING)
-        weights = spline_weights((o - cell * SPACING).astype(jnp.float32) * (1.0 / SPACING))
-        for c in range(3):
-            for k in range(4):
-                acc[c * cols + cell + k] += weights[k] * along[c * height : (c + 1) * height]
+        along = both[0:n] + both[n:]
+        for i, slot in enumerate(slots):
+            for c in range(3):
+                at = 3 * i + c
+                projected[slot, :, c * LANES : (c + 1) * LANES] = along[
+                    at * height : (at + 1) * height
+                ]
 
     def finish(d, s):
         o = edge(d, s)
@@ -390,16 +404,19 @@
                 slope[edge(d, s + 1), 2] += owed[d, at, :, 512:]
 
         if s % 2 == 0:
-            project(edge(d, s + 1))
-            project(o)
+            slot = 2 + RADIUS * (1 if d is near else 2) - s
+            project((slot - 2, slot - 1), (edge(d, s + 1), o))
 
     tables[2].wait()
     first_sums(main)
     widen(RADIUS, 0)
     middle(main)
     widen(RADIUS + 1, 1)
-    for s in range(RADIUS):
-        relay(near, s)
+    @pl.when(has(near))
+    def _():
+        for s in range(RADIUS):
+            z_copy(near, s).wait_recv()
+            spread(ext, ends, beyond(near, s))
 
     @pl.loop(0, RADIUS // 2)
     def _(i):
@@ -408,19 +425,37 @@
             widen(centre(near, s), near)
 
     def far_own(s):
-        relay(far, s)
         advance(main, far, s)
         widen(centre(far, s), far)
 
+    y_own[0].wait_recv()
+
+    @pl.when(has(near))
+    def _():
+        forward_near(1 - near).start()
+
+    relay(far, 0)
     far_own(0)
-    y_own.wait_recv()
-
-    @pl.loop(RADIUS, RADIUS + planes)
-    def _(p):
-        spread(flank, flank_ends, p)
-
-    for s in range(RADIUS):
-        relayed(near, s)
+    y_own[1].wait_recv()
+
+    @pl.when(has(far))
+    def _():
+        forward_far(1 - far).start()
+
+    relay(far, 1)
+
+    @pl.when(has(near))
+    def _():
+        forward_near(near).wait_recv()
+
+    for p in range(planes):
+        spread(flank, flank_ends, RADIUS + p)
+
+    @pl.when(has(near))
+    def _():
+        for s in range(RADIUS):
+            spread(flank, flank_ends, beyond(near, s))
+
     first_sums(side)
     totals = [totals_of(side, 0)]
     middle(side)
@@ -436,26 +471,34 @@
     def _(i):
         coefficients(near * (RADIUS + i) + far * (RADIUS + 1 - i))
 
+    relay(far, 2)
     far_own(1)
     lend_all(0, near)
     far_own(2)
     own(0, near, 0)
     gather(0, near, RADIUS + 1)
     own(0, near, 1)
+    relay(far, 3)
     far_own(3)
 
-    def far_flanks(steps):
-        totals = []
-        for s in steps:
-            relayed(far, s)
-            advance(side, far, s)
-            totals.append(totals_of(side, far))
-        widen_flanks([centre(far, s) for s in steps], totals)
-        for s in steps:
-            coefficients(centre(far, s))
-
-    far_flanks([0, 1, 2])
-    far_flanks([3])
+    @pl.when(has(far))
+    def _():
+        for s in range(RADIUS - 1):
+            y_relay(far, s).wait_recv()
+        forward_far(far).wait_recv()
+        for s in range(RADIUS):
+            spread(flank, flank_ends, beyond(far, s))
+
+    totals = []
+    for s in range(RADIUS):
+        advance(side, far, s)
+        totals.append(totals_of(side, far))
+    widen_flanks([centre(far, s) for s in range(RADIUS)], totals)
+
+    @pl.loop(0, RADIUS)
+    def _(s):
+        coefficients(centre(far, RADIUS - 1 - s))
+
     lend_all(1, far)
     local[2].wait()
     tables[0].wait()
@@ -471,22 +514,26 @@
     gather(1, far, planes - 2)
     own(1, far, planes // 2 - 1)
 
-    for d in (near, far):
-        project(edge(d, RADIUS))
-    for d in (near, far):
+    def finish_all(d):
         for s in range(RADIUS - 2, -1, -2):
             finish(d, s + 1)
             finish(d, s)
 
+    def along_z_and_y(first, count, at):
+        v = projected[first : first + count].reshape(count * height, 3 * LANES)
+        weights = by_ref[:, at : at + count * height]
+        return sum(dot(weights, piece) for piece in split(v))
+
+    project((0, 1), (edge(near, RADIUS), edge(far, RADIUS)))
+    finish_all(near)
     tables[1].wait()
+    start = along_z_and_y(0, planes - RADIUS, 0)
+    finish_all(far)
     half = points_y // 2
-    pieces = [split(acc[c * cols : (c + 1) * cols].reshape(cols * height, LANES)) for c in range(3)]
-    along_y = sum(
-        dot(by_ref[...], jnp.concatenate([piece[i] for piece in pieces], axis=1)) for i in range(2)
-    )
-    along_y = along_y[0 : cols * points_y] + along_y[cols * points_y :]
+    total = start + along_z_and_y(planes - RADIUS, RADIUS, 2 * LANES)
+    total = total[0 : cols * points_y] + total[cols * points_y :]
     for c in range(3):
-        v = along_y[:, c * LANES : (c + 1) * LANES]
+        v = total[:, c * LANES : (c + 1) * LANES]
         v = (v + turn(v, LANES // 2))[:, 0:points_x]
         for j in range(cols):
             for h in range(2):
@@ -540,7 +587,8 @@
         out_ref[owned - 1 : owned] += arrived[3, 0:1] + arrived[4, 0:1]
 
     partner.wait_send()
-    y_own.wait_send()
+    for copy in y_own:
+        copy.wait_send()
 
     @pl.when(up)
     def _():
@@ -557,14 +605,43 @@
         def _():
             for s in range(RADIUS):
                 z_copy(1 - d, s).wait_send()
-                y_relay(d, s).wait_send()
                 s_copy(1 - d, s).wait_send()
+
+    @pl.when(has(near))
+    def _():
+        forward_near(1 - near).wait_send()
+
+    @pl.when(has(far))
+    def _():
+        forward_far(1 - far).wait_send()
+        for s in range(RADIUS - 1):
+            y_relay(far, s).wait_send()
 
 
 def hi_lo(matrix):
     hi = matrix.astype(jnp.bfloat16)
     lo = (matrix - hi.astype(np.float64)).astype(jnp.bfloat16)
     return np.stack([hi, lo])
+
+
+def slab_matrix(by, planes, near):
+    position = np.arange(planes)
+    cell = position // SPACING
+    bz = np.zeros((planes, planes // SPACING + 3))
+    for k, w in enumerate(spline_weights((position - cell * SPACING) / SPACING)):
+        bz[position, cell + k] = w
+
+    def edge(d, s):
+        return planes - 1 - s if d else s
+
+    early = [edge(near, RADIUS), edge(1 - near, RADIUS)]
+    early += [edge(near, s) for s in range(RADIUS - 1, -1, -1)]
+    late = [edge(1 - near, s) for s in range(RADIUS - 1, -1, -1)]
+    blocks = []
+    for order in (early, late):
+        block = np.kron(bz[order].T, by.T)
+        blocks.append(np.pad(block, ((0, 0), (0, 2 * LANES - block.shape[1]))))
+    return np.concatenate(list(hi_lo(np.concatenate(blocks, axis=1))))
 
 
 def band_matrices(width):
@@ -587,7 +664,9 @@
     by_all = spline_matrix(gy_count * height, points_y)
     by = np.stack(
         [
-            np.concatenate(list(hi_lo(np.kron(np.eye(cols), by_all[h * height : (h + 1) * height].T))))
+            np.stack(
+                [slab_matrix(by_all[h * height : (h + 1) * height], planes, near) for near in range(2)]
+            )
             for h in range(2)
         ]
     )
@@ -606,7 +685,7 @@
         out_specs=vmem,
         scratch_shapes=[
             pltpu.VMEM(bx.shape, jnp.bfloat16),
-            pltpu.VMEM(by.shape[1:], jnp.bfloat16),
+            pltpu.VMEM(by.shape[2:], jnp.bfloat16),
             pltpu.VMEM(band.shape, jnp.bfloat16),
             pltpu.VMEM((2, planes, height, width), f32),
             pltpu.VMEM((ext_planes, height, 640), f32),
@@ -625,7 +704,7 @@
             pltpu.VMEM((planes, TILES, height, LANES), f32),
             pltpu.VMEM((2, 2, height, 640), f32),
             pltpu.VMEM((2, 2, height, 640), f32),
-            pltpu.VMEM((3 * cols, height, LANES), f32),
+            pltpu.VMEM((planes, height, 3 * LANES), f32),
             pltpu.VMEM((2, cols, 3, half, points_x), f32),
             pltpu.VMEM((5, owned, 3, half, points_x), f32),
             pltpu.SemaphoreType.DMA((6,)),
@@ -633,6 +712,8 @@
             pltpu.SemaphoreType.DMA((2, RADIUS)),
             pltpu.SemaphoreType.DMA((3, RADIUS)),
             pltpu.SemaphoreType.DMA((3, RADIUS)),
+            pltpu.SemaphoreType.DMA((2,)),
+            pltpu.SemaphoreType.DMA((2,)),
             pltpu.SemaphoreType.DMA((2, RADIUS)),
             pltpu.SemaphoreType.DMA((2, RADIUS)),
             pltpu.SemaphoreType.DMA((5,)),

time: 31.5 us -> 28.8 us (0.914)
  the two profiles are of different devices: /device:TPU:1 before, /device:TPU:17 now
where the time goes in v3:
time: 28.8 us; the launch traced here: 28.7 us
  Pallas kernels  27.2 us (94%)
  local copies, waits for them, and re-layouts  1.5 us (5%)
    pallas_call x1, Pallas kernels, local(): pl.pallas_call(body, out_shape=jax.ShapeDtypeStruct((owned, 3, half, poin...  27.2 us
    unnamed x3, local copies, waits for them, and re-layouts  1.5 us

profile of v3, /device:TPU:17, one launch (start us, length us, event | category | flops | bytes accessed | tf_op | source)
XLA Modules:
  0.0 28.7 jit_solution(785941587443407562)
XLA Ops:
  0.0 0.0 copy-start
  0.0 0.9 %copy-done = bf16[320,128]{1,0:T(8,128)(2,1)S(1)} copy-done((bf16[320,128]{1,0:T(8,128)(2,1)S(1)}, bf16[320,128]{1,0:T(8,128)(2,1)}, u32[]{:S(2)}) %copy-start) | copy-done | bytes 81944
  0.9 27.2 %shard_map.64 = f32[2,3,8,64]{3,2,1,0:T(8,128)S(1)} custom-call(f32[10,40,320]{2,1,0:T(8,128)} %fixed_ref.1, f32[10,40,320]{2,1,0:T(8,128)} %moving_ref.1, f32[3,10,40,320]{3,2,1,0:T(8,128)} %grad_ref.1, bf16[320,128]{1,0:T(8,128)(2,1)S(1)} %copy-done, bf16[2,2,160,512]{3,2,1,0:T(8,128)(2,1)} %constant.7.clone.by_hbm, bf16[256,768]{1,0:T(8,128)(2,1)} %constant.8.clone.band_hbm), custom_call_target="tpu_custom_call" | custom-call | tf_op jit(solution)/shard_map/pallas_call | solution.py:681
  28.1 0.6 %copy.8 = f32[2,3,8,64]{3,2,1,0:T(8,128)} copy(f32[2,3,8,64]{3,2,1,0:T(8,128)S(1)} %shard_map.64) | data formatting | bytes 24576
Async XLA Ops:
  0.0 0.9 %copy-start = (bf16[320,128]{1,0:T(8,128)(2,1)S(1)}, bf16[320,128]{1,0:T(8,128)(2,1)}, u32[]{:S(2)}) copy-start(bf16[320,128]{1,0:T(8,128)(2,1)} %constant.6.clone.bx_hbm) | copy-start | bytes 245764

commit v4 on v3

--- a/solution.py
+++ b/solution.py
@@ -81,15 +81,24 @@
     def beyond(d, s):
         return d * (RADIUS + planes + s) + (1 - d) * (RADIUS - 1 - s)
 
-    local = [pltpu.make_async_copy(images[i], raw.at[i], local_sem.at[i]) for i in range(2)]
-    local.append(pltpu.make_async_copy(grad_ref, grad, local_sem.at[2]))
+    def image_planes(start, count, at):
+        span = pl.ds(start, count)
+        return [
+            pltpu.make_async_copy(images[i].at[span], raw.at[i, span], local_sem.at[at + i])
+            for i in range(2)
+        ]
+
+    far_edge = far * (planes - RADIUS), RADIUS
+    others = near * RADIUS, planes - RADIUS
+    local = [image_planes(*far_edge, 0), image_planes(*others, 2)]
+    grad_copy = pltpu.make_async_copy(grad_ref, grad, local_sem.at[4])
     tables = [
-        pltpu.make_async_copy(bx_hbm, bx_ref, local_sem.at[3]),
-        pltpu.make_async_copy(by_hbm.at[g, near], by_ref, local_sem.at[4]),
-        pltpu.make_async_copy(band_hbm, band, local_sem.at[5]),
+        pltpu.make_async_copy(bx_hbm, bx_ref, local_sem.at[5]),
+        pltpu.make_async_copy(by_hbm.at[g, near], by_ref, local_sem.at[6]),
+        pltpu.make_async_copy(band_hbm, band, local_sem.at[7]),
     ]
 
-    for copy in (*local, *tables):
+    for copy in (*local[0], *local[1], tables[2]):
         copy.start()
 
     barrier = pltpu.get_barrier_semaphore()
@@ -117,22 +126,20 @@
         for ref in extended:
             ref[RADIUS + planes :] = jnp.zeros((RADIUS, *ref.shape[1:]), jnp.float32)
 
-    for i in range(2):
-        local[i].wait()
     tail = width - 256
 
     def spread(images, last, p):
         last[p] = turn(images[p, :, 512:640], -tail)
 
-    for p in range(planes):
-        at = RADIUS + p
-        ext[at, :, 0:256] = raw[0, p, :, 0:256]
-        ext[at, :, 256:512] = raw[1, p, :, 0:256]
-        ext[at, :, 512:640] = jnp.concatenate(
-            [raw[0, p, :, 256:width], raw[1, p, :, 256:width]], axis=1
-        )
-
-    pl.semaphore_wait(barrier, 1 + 2 * up.astype(jnp.int32) + 2 * down.astype(jnp.int32))
+    def pack(start, count):
+        for p in range(count):
+            p += start
+            at = RADIUS + p
+            ext[at, :, 0:256] = raw[0, p, :, 0:256]
+            ext[at, :, 256:512] = raw[1, p, :, 0:256]
+            ext[at, :, 512:640] = jnp.concatenate(
+                [raw[0, p, :, 256:width], raw[1, p, :, 256:width]], axis=1
+            )
 
     def z_copy(d, s):
         return pltpu.make_async_remote_copy(
@@ -178,13 +185,22 @@
             device_id={"gz": z + 1 - 2 * d, "gy": g}, device_id_type=MESH,
         )
 
-    for copy in y_own:
-        copy.start()
-    for d in (far, near):
+    def z_start(d):
         @pl.when(has(d))
         def _():
             for s in range(RADIUS):
                 z_copy(1 - d, s).start()
+
+    for copy in (*local[0], *local[1]):
+        copy.wait()
+    pack(0, planes)
+    pl.semaphore_wait(barrier, 1 + 2 * up.astype(jnp.int32) + 2 * down.astype(jnp.int32))
+    z_start(near)
+    z_start(far)
+    for copy in y_own:
+        copy.start()
+    for copy in (grad_copy, *tables[0:2]):
+        copy.start()
 
     for p in range(planes):
         spread(ext, ends, RADIUS + p)
@@ -268,22 +284,21 @@
     def totals_of(region, way):
         return [region[2][way, :, j].reshape(-1, LANES) for j in range(TILES)]
 
-    def widen(k, way):
-        wide = lane_windows(totals_of(main, way), 3, False)
-        for j in range(TILES):
-            for i in range(5):
-                boxes[k, i, j, HALO : HALO + height] = wide[j][i * height : (i + 1) * height]
-
-    def widen_flanks(centres, totals):
-        n = 5 * HALO
+    def widen(centres, totals):
         stacked = [jnp.concatenate([t[j] for t in totals], axis=0) for j in range(TILES)]
         wide = lane_windows(stacked, 3, False)
-        for at, k in enumerate(centres):
+        at = 0
+        for k, total in zip(centres, totals):
+            n = total[0].shape[0] // 5
             for j in range(TILES):
                 for i in range(5):
-                    v = wide[j][at * n + i * HALO : at * n + (i + 1) * HALO]
-                    boxes[k, i, j, 0:HALO] = jnp.where(g == 0, 0.0, v)
-                    boxes[k, i, j, HALO + height : rows + HALO] = jnp.where(g == 0, v, 0.0)
+                    v = wide[j][at + i * n : at + (i + 1) * n]
+                    if n == height:
+                        boxes[k, i, j, HALO : HALO + height] = v
+                    else:
+                        boxes[k, i, j, 0:HALO] = jnp.where(g == 0, 0.0, v)
+                        boxes[k, i, j, HALO + height : rows + HALO] = jnp.where(g == 0, v, 0.0)
+            at += 5 * n
 
     def coefficients(k):
         for j in range(TILES):
@@ -409,9 +424,10 @@
 
     tables[2].wait()
     first_sums(main)
-    widen(RADIUS, 0)
+    widen([RADIUS], [totals_of(main, 0)])
     middle(main)
-    widen(RADIUS + 1, 1)
+    widen([RADIUS + 1], [totals_of(main, 1)])
+
     @pl.when(has(near))
     def _():
         for s in range(RADIUS):
@@ -422,11 +438,11 @@
     def _(i):
         for s in (2 * i, 2 * i + 1):
             advance(main, near, s)
-            widen(centre(near, s), near)
+            widen([centre(near, s)], [totals_of(main, near)])
 
     def far_own(s):
         advance(main, far, s)
-        widen(centre(far, s), far)
+        widen([centre(far, s)], [totals_of(main, far)])
 
     y_own[0].wait_recv()
 
@@ -463,9 +479,7 @@
     for s in range(RADIUS):
         advance(side, near, s)
         totals.append(totals_of(side, near))
-    widen_flanks(
-        [RADIUS, RADIUS + 1, *(centre(near, s) for s in range(RADIUS))], totals
-    )
+    widen([RADIUS, RADIUS + 1, *(centre(near, s) for s in range(RADIUS))], totals)
 
     @pl.loop(0, RADIUS + 2)
     def _(i):
@@ -475,44 +489,57 @@
     far_own(1)
     lend_all(0, near)
     far_own(2)
-    own(0, near, 0)
-    gather(0, near, RADIUS + 1)
-    own(0, near, 1)
-    relay(far, 3)
-    far_own(3)
+
+    def far_sides(steps):
+        totals = []
+        for s in steps:
+            advance(side, far, s)
+            totals.append(totals_of(side, far))
+        return totals
+
+    early = range(RADIUS - 2)
+    late = range(RADIUS - 2, RADIUS)
 
     @pl.when(has(far))
     def _():
-        for s in range(RADIUS - 1):
+        for s in early:
             y_relay(far, s).wait_recv()
+            spread(flank, flank_ends, beyond(far, s))
+
+    widen([centre(far, s) for s in early], far_sides(early))
+
+    @pl.loop(0, RADIUS - 2)
+    def _(s):
+        coefficients(centre(far, s))
+
+    relay(far, RADIUS - 1)
+
+    @pl.when(has(far))
+    def _():
+        y_relay(far, RADIUS - 2).wait_recv()
         forward_far(far).wait_recv()
-        for s in range(RADIUS):
+        for s in late:
             spread(flank, flank_ends, beyond(far, s))
 
-    totals = []
-    for s in range(RADIUS):
-        advance(side, far, s)
-        totals.append(totals_of(side, far))
-    widen_flanks([centre(far, s) for s in range(RADIUS)], totals)
-
-    @pl.loop(0, RADIUS)
+    advance(main, far, RADIUS - 1)
+    widen(
+        [centre(far, s) for s in (RADIUS - 1, *late)], [totals_of(main, far), *far_sides(late)]
+    )
+
+    @pl.loop(RADIUS - 2, RADIUS)
     def _(s):
-        coefficients(centre(far, RADIUS - 1 - s))
+        coefficients(centre(far, s))
 
     lend_all(1, far)
-    local[2].wait()
+    grad_copy.wait()
     tables[0].wait()
 
-    @pl.loop(2, planes // 2)
+    @pl.loop(0, planes // 2)
     def _(i):
-        gather(0, near, RADIUS + i)
         own(0, near, i)
-        own(1, far, i - 2)
-        gather(1, far, RADIUS - 1 + i)
-
-    own(1, far, planes // 2 - 2)
-    gather(1, far, planes - 2)
-    own(1, far, planes // 2 - 1)
+        own(1, far, i)
+        gather(0, near, RADIUS + 1 + i)
+        gather(1, far, RADIUS + 1 + i)
 
     def finish_all(d):
         for s in range(RADIUS - 2, -1, -2):
@@ -707,7 +734,7 @@
             pltpu.VMEM((planes, height, 3 * LANES), f32),
             pltpu.VMEM((2, cols, 3, half, points_x), f32),
             pltpu.VMEM((5, owned, 3, half, points_x), f32),
-            pltpu.SemaphoreType.DMA((6,)),
+            pltpu.SemaphoreType.DMA((8,)),
             pltpu.SemaphoreType.DMA((2, RADIUS)),
             pltpu.SemaphoreType.DMA((2, RADIUS)),
             pltpu.SemaphoreType.DMA((3, RADIUS)),
@@ -720,7 +747,7 @@
             pltpu.SemaphoreType.DMA((5,)),
         ],
         compiler_params=pltpu.CompilerParams(
-            collective_id=0, has_side_effects=True, vmem_limit_bytes=56450000
+            collective_id=0, has_side_effects=True, vmem_limit_bytes=56510000
         ),
     )(fixed_image, moving_image, moving_grad, jnp.asarray(bx), jnp.asarray(by), jnp.asarray(band))
 

time: 28.8 us -> 27.7 us (0.962)
  the two profiles are of different devices: /device:TPU:17 before, /device:TPU:1 now
where the time goes in v4:
time: 27.7 us; the launch traced here: 27.4 us
  Pallas kernels  26.8 us (97%)
  local copies, waits for them, and re-layouts  0.61 us (2%)
    pallas_call x1, Pallas kernels, local(): pl.pallas_call(body, out_shape=jax.ShapeDtypeStruct((owned, 3, half, poin...  26.8 us
    unnamed x1, local copies, waits for them, and re-layouts  0.61 us

profile of v4, /device:TPU:1, one launch (start us, length us, event | category | flops | bytes accessed | tf_op | source)
XLA Modules:
  0.0 27.4 jit_solution(8511118342737405266)
XLA Ops:
  0.0 26.8 %shard_map.64 = f32[2,3,8,64]{3,2,1,0:T(8,128)S(1)} custom-call(f32[10,40,320]{2,1,0:T(8,128)} %fixed_ref.1, f32[10,40,320]{2,1,0:T(8,128)} %moving_ref.1, f32[3,10,40,320]{3,2,1,0:T(8,128)} %grad_ref.1, bf16[320,128]{1,0:T(8,128)(2,1)} %constant.6.clone.bx_hbm, bf16[2,2,160,512]{3,2,1,0:T(8,128)(2,1)} %constant.7.clone.by_hbm, ...), custom_call_target="tpu_custom_call" | custom-call | tf_op jit(solution)/shard_map/pallas_call | solution.py:708
  26.8 0.6 %copy.8 = f32[2,3,8,64]{3,2,1,0:T(8,128)} copy(f32[2,3,8,64]{3,2,1,0:T(8,128)S(1)} %shard_map.64) | data formatting | bytes 24576

commit v5 on v4

--- a/solution.py
+++ b/solution.py
@@ -174,7 +174,8 @@
         return forward(d, pl.ds(src, RADIUS), pl.ds(d * (RADIUS + planes), RADIUS))
 
     def forward_far(d):
-        return forward(d, RADIUS + edge(1 - d, RADIUS - 1), beyond(d, RADIUS - 1))
+        src = RADIUS + (1 - d) * (planes - RADIUS) + d * (RADIUS - 2)
+        return forward(d, pl.ds(src, 2), pl.ds(d * (RADIUS + planes + 2), 2))
 
     def s_copy(d, s):
         lane = slice(0, 256) if s % 2 else slice(256, packed)
@@ -209,7 +210,7 @@
         @pl.when(has(d))
         def _():
             z_copy(d, s).wait_recv()
-            if s < RADIUS - 1:
+            if s < RADIUS - 2:
                 y_relay(d, s).start()
             spread(ext, ends, beyond(d, s))
 
@@ -253,13 +254,13 @@
     lane = lax.broadcasted_iota(jnp.int32, (rows, LANES), 1) - RADIUS
     in_rows = (row >= 0) & (row < 2 * height)
 
-    def first_sums(region):
+    def first_sums(region, unroll=1):
         total = region[2]
         for j in range(TILES):
             def add(p, totals):
                 return tuple(a + b for a, b in zip(totals, fields(region, RADIUS + p, j)))
 
-            totals = lax.fori_loop(1, HALO + 1, add, fields(region, RADIUS, j))
+            totals = lax.fori_loop(1, HALO + 1, add, fields(region, RADIUS, j), unroll=unroll)
             for i in range(5):
                 total[0, i, j] = totals[i]
                 total[1, i, j] = totals[i]
@@ -472,7 +473,7 @@
         for s in range(RADIUS):
             spread(flank, flank_ends, beyond(near, s))
 
-    first_sums(side)
+    first_sums(side, HALO)
     totals = [totals_of(side, 0)]
     middle(side)
     totals.append(totals_of(side, 1))
@@ -486,9 +487,7 @@
         coefficients(near * (RADIUS + i) + far * (RADIUS + 1 - i))
 
     relay(far, 2)
-    far_own(1)
     lend_all(0, near)
-    far_own(2)
 
     def far_sides(steps):
         totals = []
@@ -506,7 +505,11 @@
             y_relay(far, s).wait_recv()
             spread(flank, flank_ends, beyond(far, s))
 
-    widen([centre(far, s) for s in early], far_sides(early))
+    far_main = []
+    for s in (1, 2):
+        advance(main, far, s)
+        far_main.append(totals_of(main, far))
+    widen([centre(far, s) for s in (1, 2, *early)], [*far_main, *far_sides(early)])
 
     @pl.loop(0, RADIUS - 2)
     def _(s):
@@ -516,7 +519,6 @@
 
     @pl.when(has(far))
     def _():
-        y_relay(far, RADIUS - 2).wait_recv()
         forward_far(far).wait_recv()
         for s in late:
             spread(flank, flank_ends, beyond(far, s))
@@ -555,9 +557,13 @@
     finish_all(near)
     tables[1].wait()
     start = along_z_and_y(0, planes - RADIUS, 0)
-    finish_all(far)
+    finish(far, 3)
+    finish(far, 2)
+    start += along_z_and_y(planes - RADIUS, 2, 2 * LANES)
+    finish(far, 1)
+    finish(far, 0)
     half = points_y // 2
-    total = start + along_z_and_y(planes - RADIUS, RADIUS, 2 * LANES)
+    total = start + along_z_and_y(planes - RADIUS + 2, 2, 3 * LANES)
     total = total[0 : cols * points_y] + total[cols * points_y :]
     for c in range(3):
         v = total[:, c * LANES : (c + 1) * LANES]
@@ -641,7 +647,7 @@
     @pl.when(has(far))
     def _():
         forward_far(1 - far).wait_send()
-        for s in range(RADIUS - 1):
+        for s in range(RADIUS - 2):
             y_relay(far, s).wait_send()
 
 
@@ -665,9 +671,9 @@
     early += [edge(near, s) for s in range(RADIUS - 1, -1, -1)]
     late = [edge(1 - near, s) for s in range(RADIUS - 1, -1, -1)]
     blocks = []
-    for order in (early, late):
+    for order, lanes in ((early, 2 * LANES), (late[0:2], LANES), (late[2:4], LANES)):
         block = np.kron(bz[order].T, by.T)
-        blocks.append(np.pad(block, ((0, 0), (0, 2 * LANES - block.shape[1]))))
+        blocks.append(np.pad(block, ((0, 0), (0, lanes - block.shape[1]))))
     return np.concatenate(list(hi_lo(np.concatenate(blocks, axis=1))))
 
 

time: 27.7 us -> 27.3 us (0.986)
  Pallas kernels: 26.8 us -> 26.5 us
    pallas_call x1, Pallas kernels: 26.8 us -> 26.5 us  [local(): pl.pallas_call(body, out_shape=jax.ShapeDtypeStruct((owned, 3, half, poin...]
where the time goes in v5:
time: 27.3 us; the launch traced here: 27.1 us
  Pallas kernels  26.5 us (97%)
  local copies, waits for them, and re-layouts  0.61 us (2%)
    pallas_call x1, Pallas kernels, local(): pl.pallas_call(body, out_shape=jax.ShapeDtypeStruct((owned, 3, half, poin...  26.5 us
    unnamed x1, local copies, waits for them, and re-layouts  0.61 us

profile of v5, /device:TPU:1, one launch (start us, length us, event | category | flops | bytes accessed | tf_op | source)
XLA Modules:
  0.0 27.1 jit_solution(3120718775948450651)
XLA Ops:
  0.0 26.5 %shard_map.64 = f32[2,3,8,64]{3,2,1,0:T(8,128)S(1)} custom-call(f32[10,40,320]{2,1,0:T(8,128)} %fixed_ref.1, f32[10,40,320]{2,1,0:T(8,128)} %moving_ref.1, f32[3,10,40,320]{3,2,1,0:T(8,128)} %grad_ref.1, bf16[320,128]{1,0:T(8,128)(2,1)} %constant.6.clone.bx_hbm, bf16[2,2,160,512]{3,2,1,0:T(8,128)(2,1)} %constant.7.clone.by_hbm, ...), custom_call_target="tpu_custom_call" | custom-call | tf_op jit(solution)/shard_map/pallas_call | solution.py:714
  26.5 0.6 %copy.8 = f32[2,3,8,64]{3,2,1,0:T(8,128)} copy(f32[2,3,8,64]{3,2,1,0:T(8,128)S(1)} %shard_map.64) | data formatting | bytes 24576

commit v6 on v5

--- a/solution.py
+++ b/solution.py
@@ -109,9 +109,8 @@
             pl.semaphore_signal(barrier, 1, device_id={"gz": z + dz, "gy": gy}, device_id_type=MESH)
 
     pl.semaphore_signal(barrier, 1, device_id={"gz": z, "gy": other}, device_id_type=MESH)
-    for gy in (g, other):
-        greet(up, 1, gy)
-        greet(down, -1, gy)
+    greet(up, 1, g)
+    greet(down, -1, g)
 
     packed = ext.shape[2]
     extended = (ext, ends, flank, flank_ends)
@@ -195,7 +194,7 @@
     for copy in (*local[0], *local[1]):
         copy.wait()
     pack(0, planes)
-    pl.semaphore_wait(barrier, 1 + 2 * up.astype(jnp.int32) + 2 * down.astype(jnp.int32))
+    pl.semaphore_wait(barrier, 1 + up.astype(jnp.int32) + down.astype(jnp.int32))
     z_start(near)
     z_start(far)
     for copy in y_own:
@@ -345,7 +344,7 @@
             for j in range(TILES):
                 ksum[slot, i, j] += coef[i, edge(d, s), j]
 
-    def lend_all(slot, d):
+    def lend_all(slot, d, after_first=lambda: None):
         for i in range(3):
             ksum[slot, i] = coef[i, edge(d, 0)]
 
@@ -363,10 +362,13 @@
                     lent[d, at, :, 384:512] = b
                     lent[d, at, :, 512:] = jnp.where(spot < tail, first, turn(c, tail))
                 s_copy(1 - d, s).start()
+                if s == RADIUS - 1:
+                    after_first()
                 gather(slot, d, RADIUS - s)
 
         @pl.when(jnp.logical_not(has(d)))
         def _():
+            after_first()
             for s in range(RADIUS):
                 gather(slot, d, RADIUS - s)
 
@@ -528,11 +530,8 @@
         [centre(far, s) for s in (RADIUS - 1, *late)], [totals_of(main, far), *far_sides(late)]
     )
 
-    @pl.loop(RADIUS - 2, RADIUS)
-    def _(s):
-        coefficients(centre(far, s))
-
-    lend_all(1, far)
+    coefficients(centre(far, RADIUS - 1))
+    lend_all(1, far, lambda: coefficients(centre(far, RADIUS - 2)))
     grad_copy.wait()
     tables[0].wait()
 

time: 27.3 us -> 27 us (0.989)
  Pallas kernels: 26.5 us -> 26.2 us
where the time goes in v6:
time: 27 us; the launch traced here: 26.8 us
  Pallas kernels  26.2 us (97%)
  local copies, waits for them, and re-layouts  0.61 us (2%)
    pallas_call x1, Pallas kernels, local(): pl.pallas_call(body, out_shape=jax.ShapeDtypeStruct((owned, 3, half, poin...  26.2 us
    unnamed x1, local copies, waits for them, and re-layouts  0.61 us

profile of v6, /device:TPU:1, one launch (start us, length us, event | category | flops | bytes accessed | tf_op | source)
XLA Modules:
  0.0 26.8 jit_solution(6695372980671958653)
XLA Ops:
  0.0 26.2 %shard_map.64 = f32[2,3,8,64]{3,2,1,0:T(8,128)S(1)} custom-call(f32[10,40,320]{2,1,0:T(8,128)} %fixed_ref.1, f32[10,40,320]{2,1,0:T(8,128)} %moving_ref.1, f32[3,10,40,320]{3,2,1,0:T(8,128)} %grad_ref.1, bf16[320,128]{1,0:T(8,128)(2,1)} %constant.6.clone.bx_hbm, bf16[2,2,160,512]{3,2,1,0:T(8,128)(2,1)} %constant.7.clone.by_hbm, ...), custom_call_target="tpu_custom_call" | custom-call | tf_op jit(solution)/shard_map/pallas_call | solution.py:713
  26.2 0.6 %copy.8 = f32[2,3,8,64]{3,2,1,0:T(8,128)} copy(f32[2,3,8,64]{3,2,1,0:T(8,128)S(1)} %shard_map.64) | data formatting | bytes 24576
